TPU v7x, 32 devices: a whole 2x2x4 slice. The times are simulated.
32 devices in a mesh: sub: 8 (over z, y), inner: 4 (over x, core).
Axes of the slice: x: 2, y: 2, z: 4, core: 2. Of those that a mesh axis runs over, the one named last changes fastest.
Arguments:
- solution: float32 [32, 3, 32, 16, 128], P(None, None, 'sub', 'inner'), may hold values from -6 to 6
- residual: float32 [32, 3, 32, 16, 128], P(None, None, 'sub', 'inner'), may hold values from -6 to 6
- direction: float32 [32, 3, 32, 16, 128], P(None, None, 'sub', 'inner'), may hold values from -6 to 6
- mass: float32 [32, 16, 128], P('sub', 'inner'), may hold values from 0.2 to 5
- coarse_basis: float32 [32, 3, 32, 16, 128], P(None, None, 'sub', 'inner'), may hold values from -1 to 1
- line_inverse: float32 [8, 4, 128, 128], P('sub', 'inner'), may hold values from -1.5 to 1.5
- coarse_factor: float32 [1024, 1024], P(('sub', 'inner')), may hold values from -1 to 1
Outputs:
- new_solution: float32 [32, 3, 32, 16, 128], P(None, None, 'sub', 'inner')
- new_residual: float32 [32, 3, 32, 16, 128], P(None, None, 'sub', 'inner')
- new_direction: float32 [32, 3, 32, 16, 128], P(None, None, 'sub', 'inner')
All inputs are finite; a program needn't handle non-finite values.
Results may differ from a plain program's by a relative error of at most 0.00017.
Values sent between devices are 32-bit elements; how exact they have to be, the bound alone decides.
A program may use at most 64 MiB of HBM per device.

v0:
```python
import functools

import jax
import jax.numpy as jnp
from jax import lax
from jax.experimental import pallas as pl
from jax.experimental.pallas import tpu as pltpu
from jax.sharding import PartitionSpec as P

exact_mode = lax.Precision.HIGHEST
close_mode = lax.Precision.HIGH


def sum_kernel(stages, wide_ref, small_ref, wide_out, small_out, *scratch):
    count = len(stages)
    total, held, small_parts, small_landed = scratch[:4]
    landed = scratch[4 : 4 + count]
    send_sem, recv_sem, small_send, small_recv, back_send, back_recv = scratch[4 + count :]
    bits, partners = ([], [])
    for axis, stride in stages:
        index = lax.axis_index(axis)
        bit = (index // stride) % 2
        bits.append(bit)
        partners.append({axis: index + stride * (1 - 2 * bit)})
    barrier = pltpu.get_barrier_semaphore()
    for partner in partners:
        pl.semaphore_signal(barrier, inc=1, device_id=partner, device_id_type=pl.DeviceIdType.MESH)
    pl.semaphore_wait(barrier, count)

    width = wide_ref.shape[0]
    base = 0
    for t in range(count):
        half = width // 2
        keep = pl.multiple_of(base + bits[t] * half, 8)
        give = pl.multiple_of(base + (1 - bits[t]) * half, 8)
        source = wide_ref if t == 0 else total
        small_source = small_ref if t == 0 else small_parts.at[t - 1]
        small_copy = pltpu.make_async_remote_copy(
            src_ref=small_source,
            dst_ref=small_landed.at[t],
            send_sem=small_send.at[t],
            recv_sem=small_recv.at[t],
            device_id=partners[t],
            device_id_type=pl.DeviceIdType.MESH,
        )
        copy = pltpu.make_async_remote_copy(
            src_ref=source.at[pl.ds(give, half)],
            dst_ref=landed[t],
            send_sem=send_sem.at[t],
            recv_sem=recv_sem.at[t],
            device_id=partners[t],
            device_id_type=pl.DeviceIdType.MESH,
        )
        small_copy.start()
        copy.start()
        small_copy.wait()
        small_sum = small_source[...] + small_landed[t]
        if t < count - 1:
            small_parts[t] = small_sum
        else:
            small_out[...] = small_sum
        copy.wait()
        target = total if t < count - 1 else held
        target[pl.ds(keep, half), :] = source[pl.ds(keep, half), :] + landed[t][...]
        base = base + bits[t] * half
        width = half
    for t in reversed(range(count)):
        mine = pl.ds(pl.multiple_of(base, 8), width)
        copy = pltpu.make_async_remote_copy(
            src_ref=held.at[mine],
            dst_ref=held.at[mine],
            send_sem=back_send.at[t],
            recv_sem=back_recv.at[t],
            device_id=partners[t],
            device_id_type=pl.DeviceIdType.MESH,
        )
        copy.start()
        copy.wait()
        base = base - bits[t] * width
        width = width * 2
    wide_out[...] = held[...]


def sum_everywhere(wide, small, axes):
    stages = []
    for axis in axes:
        stride = 1
        while stride < lax.axis_size(axis):
            stages.append((axis, stride))
            stride *= 2
    count = len(stages)
    rows, lanes = wide.shape
    vmem = pl.BlockSpec(memory_space=pltpu.VMEM)
    dma = pltpu.SemaphoreType.DMA((count,))
    return pl.pallas_call(
        functools.partial(sum_kernel, tuple(stages)),
        out_shape=(
            jax.ShapeDtypeStruct(wide.shape, wide.dtype),
            jax.ShapeDtypeStruct(small.shape, small.dtype),
        ),
        in_specs=[vmem, vmem],
        out_specs=(vmem, vmem),
        scratch_shapes=[
            pltpu.VMEM(wide.shape, wide.dtype),
            pltpu.VMEM(wide.shape, wide.dtype),
            pltpu.VMEM((count,) + small.shape, small.dtype),
            pltpu.VMEM((count,) + small.shape, small.dtype),
            *[pltpu.VMEM((rows >> (t + 1), lanes), wide.dtype) for t in range(count)],
            dma,
            dma,
            dma,
            dma,
            dma,
            dma,
        ],
        compiler_params=pltpu.CompilerParams(collective_id=0, has_side_effects=True),
    )(wide, small)


def with_halo(array, sides, width):
    for axis, dim in sides:
        count, length = (lax.axis_size(axis), array.shape[dim])
        up = [(i, (i + 1) % count) for i in range(count - 1)]
        down = [(j, i) for i, j in up]
        last = lax.slice_in_dim(array, length - width, length, axis=dim)
        initial = lax.slice_in_dim(array, 0, width, axis=dim)
        before = lax.ppermute(last, axis, up)
        after = lax.ppermute(initial, axis, down)
        array = jnp.concatenate([before, array, after], axis=dim)
    return array


def shifted(padded, which, offset):
    window = [slice(None), slice(None)]
    for place in (2, 3, 4):
        length = padded.shape[place]
        if place == which:
            window.append(slice(2 + offset, length - 2 + offset))
        else:
            window.append(slice(2, length - 2))
    return padded[tuple(window)]


def operate(direction, mass):
    widened = with_halo(direction, (("sub", 2), ("inner", 3)), 2)
    padded = jnp.pad(widened, ((0, 0), (0, 0), (0, 0), (0, 0), (2, 2)))
    center = shifted(padded, 2, 0)
    nearby = jnp.zeros_like(center)
    farther = jnp.zeros_like(center)
    for which in (2, 3, 4):
        nearby = nearby + shifted(padded, which, 1) + shifted(padded, which, -1)
        farther = farther + shifted(padded, which, 2) + shifted(padded, which, -2)
    return (mass + 7.5) * center - 4.0 / 3.0 * nearby + 1.0 / 12.0 * farther


def spd_solve(lower, rhs):
    middle = lax.linalg.triangular_solve(lower, rhs, left_side=True, lower=True)
    return lax.linalg.triangular_solve(lower, middle, left_side=True, lower=True, transpose_a=True)


def along_lines(flat, inverse):
    lines = flat.reshape(-1, inverse.shape[0])
    return jnp.dot(lines, inverse.T, precision=close_mode).reshape(flat.shape)


def product(left, right):
    return jnp.dot(left, right.T, precision=exact_mode)


def on_device(solution, residual, direction, mass, coarse_basis, line_inverse, coarse_factor):
    directions = direction.shape[0]
    shape = direction.shape
    inverse = line_inverse[0, 0]
    image = operate(direction, mass)
    flat_p = direction.reshape(directions, -1)
    flat_q = image.reshape(directions, -1)
    flat_r = residual.reshape(directions, -1)
    flat_s = solution.reshape(directions, -1)
    basis_flat = coarse_basis.reshape(coarse_basis.shape[0], -1)
    lined_r = along_lines(flat_r, inverse)
    lined_q = along_lines(flat_q, inverse)
    rhs_r = product(basis_flat, flat_r)
    rhs_q = product(basis_flat, flat_q)
    small = jnp.concatenate(
        [product(flat_p, flat_q), product(flat_p, flat_r), product(flat_q, lined_r), product(flat_q, lined_q)], axis=1
    )
    rhs_both = jnp.concatenate([rhs_r, rhs_q], axis=1)
    half = coarse_factor.shape[1] // 2
    wide = jnp.concatenate(
        [
            jnp.dot(coarse_factor[:, :half].T, rhs_both, precision=exact_mode),
            jnp.dot(coarse_factor[:, half:].T, rhs_both, precision=exact_mode),
        ],
        axis=1,
    )
    wide, small = sum_everywhere(wide, small, ("inner", "sub"))
    gram_pq, proj_pr, image_lined_r, image_lined_q = jnp.split(small, 4, axis=1)
    mids = jnp.concatenate([wide[:, : 2 * directions], wide[:, 2 * directions :]], axis=0)
    mid_r, mid_q = (mids[:, :directions], mids[:, directions:])
    lower = jnp.linalg.cholesky(gram_pq)
    alpha_mix = spd_solve(lower, proj_pr)
    flat_new = flat_r - jnp.dot(alpha_mix.T, flat_q, precision=close_mode)
    local_part = lined_r - jnp.dot(alpha_mix.T, lined_q, precision=close_mode)
    coarse_mid = mid_r - jnp.dot(mid_q, alpha_mix, precision=exact_mode)
    coarse_sol = jnp.dot(coarse_factor, coarse_mid, precision=exact_mode)
    precond = local_part + jnp.dot(coarse_sol.T, basis_flat, precision=close_mode)
    cross_qz = (
        image_lined_r
        - jnp.dot(image_lined_q, alpha_mix, precision=exact_mode)
        + jnp.dot(mid_q.T, coarse_mid, precision=exact_mode)
    )
    new_solution = flat_s + jnp.dot(alpha_mix.T, flat_p, precision=close_mode)
    beta_mix = -spd_solve(lower, cross_qz)
    new_direction = precond + jnp.dot(beta_mix.T, flat_p, precision=close_mode)
    return (new_solution.reshape(shape), flat_new.reshape(shape), new_direction.reshape(shape))


def solution(mesh):
    placed = (
        P(None, None, "sub", "inner", None),
        P(None, None, "sub", "inner", None),
        P(None, None, "sub", "inner", None),
        P("sub", "inner", None),
        P(None, None, "sub", "inner", None),
        P("sub", "inner", None, None),
        P(("sub", "inner"), None),
    )
    return jax.shard_map(
        on_device,
        mesh=mesh,
        in_specs=placed,
        out_specs=(
            P(None, None, "sub", "inner", None),
            P(None, None, "sub", "inner", None),
            P(None, None, "sub", "inner", None),
        ),
        check_vma=False,
    )
```

profile of v0, /device:TPU:0, one launch (start us, length us, event | category | flops | bytes accessed | tf_op | source)
XLA Modules:
  0.0 123.4 jit_solution(9809226903969542695)
XLA Ops:
  0.6 1.2 fusion.45
  2.0 1.4 %collective-permute-start = (f32[32,3,2,4,128]{4,0,3,2,1:T(8,128)S(1)}, f32[32,3,2,4,128]{4,0,3,2,1:T(8,128)S(1)}, u32[]{:S(2)}, u32[]{:S(2)}) collective-permute-start(f32[32,3,2,4,128]{4,0,3,2,1:T(8,128)S(1)} %copy.115), channel_id=1, source_target_pairs={{4,0},{8,4},{12,8},{16,12},{20,16},{24,20},{28,24},{5,1},{9,5},{13... | collective-permute-start | bytes 1179656 | tf_op jit(solution)/shard_map/ppermute | solution.py:128
  4.2 6.3 %collective-permute-start.1 = (f32[32,3,2,4,128]{4,0,3,2,1:T(8,128)}, f32[32,3,2,4,128]{4,0,3,2,1:T(8,128)}, u32[]{:S(2)}, u32[]{:S(2)}) collective-permute-start(f32[32,3,2,4,128]{4,0,3,2,1:T(8,128)} %copy.114), channel_id=1, source_target_pairs={{0,4},{4,8},{8,12},{12,16},{16,20},{20,24},{24,28},{1,5},{5,9},{9,... | collective-permute-start | bytes 1179656 | tf_op jit(solution)/shard_map/ppermute | solution.py:127
  10.5 1.3 %copy.68 = f32[32,3,4,4,128]{4,2,3,1,0:T(4,128)S(1)} copy(f32[32,3,4,4,128]{4,3,2,1,0:T(4,128)} %param.13) | data formatting | bytes 1572864 | tf_op args[2]
  11.9 2.4 %reshape.59 = f32[32,6144]{1,0:T(8,128)} reshape(f32[32,3,4,4,128]{4,3,2,1,0:T(4,128)} %param.13) | data formatting | bytes 1572864 | tf_op jit(solution)/shard_map/reshape | solution.py:175
  14.2 1.9 %collective-permute-done = f32[32,3,2,4,128]{4,0,3,2,1:T(8,128)S(1)} collective-permute-done((f32[32,3,2,4,128]{4,0,3,2,1:T(8,128)S(1)}, f32[32,3,2,4,128]{4,0,3,2,1:T(8,128)S(1)}, u32[]{:S(2)}, u32[]{:S(2)}) %collective-permute-start) | collective-permute-done | bytes 393248 | tf_op jit(solution)/shard_map/ppermute | solution.py:128
  16.4 8.4 %collective-permute-done.1 = f32[32,3,2,4,128]{4,0,3,2,1:T(8,128)} collective-permute-done((f32[32,3,2,4,128]{4,0,3,2,1:T(8,128)}, f32[32,3,2,4,128]{4,0,3,2,1:T(8,128)}, u32[]{:S(2)}, u32[]{:S(2)}) %collective-permute-start.1) | collective-permute-done | bytes 393248 | tf_op jit(solution)/shard_map/ppermute | solution.py:127
  24.8 1.3 %copy.73 = f32[32,3,2,4,128]{4,2,3,1,0:T(2,128)S(1)} copy(f32[32,3,2,4,128]{4,0,3,2,1:T(8,128)} %collective-permute-done.1) | data formatting | bytes 786432 | tf_op jit(solution)/shard_map/ppermute | solution.py:127
  26.9 1.3 %fusion.44 = (f32[32,3,8,2,128]{4,2,3,1,0:T(8,128)}, f32[32,3,8,2,128]{4,2,3,1,0:T(8,128)}) fusion(f32[32,3,8,4,128]{4,2,3,1,0:T(8,128)S(1)} %pad_maximum_fusion), kind=kLoop, calls=%fused_computation.91 | loop fusion | bytes 3145728 | tf_op jit(solution)/shard_map/slice | solution.py:125
  28.1 1.3 %collective-permute-start.2 = (f32[32,3,8,2,128]{4,2,3,1,0:T(8,128)}, f32[32,3,8,2,128]{4,2,3,1,0:T(8,128)}, u32[]{:S(2)}, u32[]{:S(2)}) collective-permute-start(f32[32,3,8,2,128]{4,2,3,1,0:T(8,128)} %get-tuple-element.10), channel_id=1, source_target_pairs={{1,0},{2,1},{3,2},{5,4},{6,5},{7,6},{9,8},{10,9},{11,10},{13,12},{... | collective-permute-start | bytes 2359304 | tf_op jit(solution)/shard_map/ppermute | solution.py:128
  29.4 3.9 %collective-permute-start.3 = (f32[32,3,8,2,128]{4,2,3,1,0:T(8,128)}, f32[32,3,8,2,128]{4,2,3,1,0:T(8,128)}, u32[]{:S(2)}, u32[]{:S(2)}) collective-permute-start(f32[32,3,8,2,128]{4,2,3,1,0:T(8,128)} %get-tuple-element.9), channel_id=1, source_target_pairs={{0,1},{1,2},{2,3},{4,5},{5,6},{6,7},{8,9},{9,10},{10,11},{12,13},{... | collective-permute-start | bytes 2359304 | tf_op jit(solution)/shard_map/ppermute | solution.py:127
  33.4 1.3 %reshape.61 = f32[32,6144]{1,0:T(8,128)} reshape(f32[32,3,4,4,128]{4,3,2,1,0:T(4,128)S(1)} %copy-done.2) | data formatting | bytes 1572864 | tf_op jit(solution)/shard_map/reshape | solution.py:177
  34.7 1.4 %fusion.23 = f32[1536,128]{1,0:T(8,128)} fusion(f32[1536,128]{1,0:T(8,128)S(1)} %bitcast.76, f32[1,1,128,128]{3,2,1,0:T(8,128)S(1)} %copy-done), kind=kOutput, calls=%fused_computation.61 | convolution fusion | flops 150994944 | bytes 1638400 | tf_op jit(solution)/shard_map/dot_general | solution.py:163
  36.0 2.1 %reshape.57 = f32[32,6144]{1,0:T(8,128)} reshape(f32[1536,128]{1,0:T(8,128)} %fusion.23) | data formatting | bytes 1572864 | tf_op jit(solution)/shard_map/reshape | solution.py:163
  38.2 1.2 %reshape.63 = f32[32,6144]{1,0:T(8,128)} reshape(f32[32,3,4,4,128]{4,3,2,1,0:T(4,128)S(1)} %copy-done.3) | data formatting | bytes 1572864 | tf_op jit(solution)/shard_map/reshape | solution.py:179
  39.4 2.4 %reshape.55 = f32[32,6144]{1,0:T(8,128)} reshape(f32[32,3,4,4,128]{4,3,2,1,0:T(4,128)} %param.11) | data formatting | bytes 1572864 | tf_op jit(solution)/shard_map/reshape | solution.py:178
  44.1 5.9 %select_maximum_fusion = f32[32,3,8,8,132]{4,2,3,1,0:T(8,128)S(1)} fusion(f32[32,3,8,2,128]{4,2,3,1,0:T(8,128)} %collective-permute-done.2, f32[32,3,8,2,128]{4,2,3,1,0:T(8,128)} %collective-permute-done.3, f32[32,3,2,4,128]{4,2,3,1,0:T(2,128)} %copy-done.6, f32[32,3,4,4,128]{4,2,3,1,0:T(4,128)S(1)} %copy.68, f32[32,3,2,4,128]{4,2,3,1,0:T(2,128)} %copy-done.8), kind=kLoop, calls=%fused_computation.7 | loop fusion | flops 9732096 | bytes 6389760 | tf_op jit(solution)/shard_map/concatenate | solution.py:129
  50.0 5.3 %fusion.9 = f32[32,3,4,4,128]{4,2,3,1,0:T(4,128)S(1)} fusion(f32[32,3,2,4,128]{4,2,3,1,0:T(2,128)S(1)} %copy-done.9, f32[32,3,4,4,128]{4,2,3,1,0:T(4,128)S(1)} %copy.68, f32[32,3,2,4,128]{4,2,3,1,0:T(2,128)S(1)} %copy-done.7, f32[32,3,8,8,132]{4,2,3,1,0:T(8,128)S(1)} %select_maximum_fusion, f32[32,3,8,2,128]{4,2,3,1,0:T(8,128)} %collective-permute-done.3, ...), kind=kLoop, calls=%fused_computation.35 | loop fusion | flops 6094848 | bytes 7086080 | tf_op jit(solution)/shard_map/add | solution.py:153
  56.8 1.2 convolution_bitcast_fusion.4
  58.6 1.3 %convolution_bitcast_fusion.1 = f32[512,64]{1,0:T(8,128)} fusion(f32[32,1024]{1,0:T(8,128)S(1)} %copy-done.12, f32[32,32]{1,0:T(8,128)S(1)} %convolution_bitcast_fusion.4, f32[32,32]{1,0:T(8,128)S(1)} %convolution_bitcast_fusion.5), kind=kOutput, calls=%fused_computation.19 | convolution fusion | flops 12584960 | bytes 229376 | tf_op jit(solution)/shard_map/dot_general | solution.py:191
  60.3 1.4 %fusion.21 = f32[1536,128]{1,0:T(8,128)} fusion(f32[1536,128]{1,0:T(8,128)S(1)} %bitcast.77, f32[1,1,128,128]{3,2,1,0:T(8,128)S(1)} %copy-done), kind=kOutput, calls=%fused_computation.59 | convolution fusion | flops 150994944 | bytes 1638400 | tf_op jit(solution)/shard_map/dot_general | solution.py:163
  61.6 1.3 %reshape.58 = f32[32,6144]{1,0:T(8,128)S(1)} reshape(f32[1536,128]{1,0:T(8,128)} %fusion.21) | data formatting | bytes 1572864 | tf_op jit(solution)/shard_map/reshape | solution.py:163
  63.7 2.0 %fusion.47 = f32[32,32]{1,0:T(8,128)S(1)} fusion(f32[32,6144]{1,0:T(8,128)S(1)} %reshape.56, f32[32,6144]{1,0:T(8,128)} %reshape.57), kind=kOutput, calls=%fused_computation.94 | convolution fusion | flops 75497472 | bytes 1576960 | tf_op jit(solution)/shard_map/dot_general | solution.py:167
  65.6 1.8 %pad_maximum_fusion.12.wide_ref = f32[512,128]{1,0:T(8,128)} fusion(f32[512,64]{1,0:T(8,128)S(1)} %convolution_bitcast_fusion, f32[512,64]{1,0:T(8,128)} %convolution_bitcast_fusion.1), kind=kLoop, calls=%fused_computation.58 | loop fusion | flops 65536 | bytes 524288 | tf_op jit(solution)/shard_map/concatenate | solution.py:189
  68.1 32.2 %shard_map.94 = (f32[512,128]{1,0:T(8,128)}, f32[32,128]{1,0:T(8,128)}) custom-call(f32[512,128]{1,0:T(8,128)} %pad_maximum_fusion.12.wide_ref, f32[32,128]{1,0:T(8,128)} %pad_maximum_fusion.14.small_ref), custom_call_target="tpu_custom_call" | custom-call | tf_op jit(solution)/shard_map/pallas_call | solution.py:95
  101.2 2.9 %cholesky.18 = f32[32,32]{1,0:T(8,128)S(1)} custom-call(f32[32,32]{1,0:T(8,128)S(1)} %fusion.35), custom_call_target="Cholesky" | custom-call | tf_op jit(solution)/shard_map/jit(cholesky)/cholesky | solution.py:200
  105.5 2.4 %custom-call.12 = f32[1,32,32]{1,2,0:T(8,128)S(1)} custom-call(f32[1,32,32]{2,1,0:T(8,128)S(1)} %fusion.27), custom_call_target="InvertDiagBlocksLowerTriangular" | custom-call | tf_op jit(solution)/shard_map/triangular_solve/custom-call.2 | solution.py:158
  112.5 1.9 %fusion.49 = f32[32,32]{1,0:T(8,128)S(1)} fusion(f32[1024,32]{1,0:T(8,128)S(1)} %convolution_subtract_fusion.2, f32[32,1024]{1,0:T(8,128)} %param.17), kind=kOutput, calls=%fused_computation.96 | convolution fusion | flops 12582912 | bytes 266240 | tf_op jit(solution)/shard_map/dot_general | solution.py:205
  117.0 1.4 %reshape.64 = f32[32,3,4,4,128]{4,3,2,1,0:T(4,128)} reshape(f32[32,6144]{1,0:T(8,128)S(1)} %convolution_add_fusion) | data formatting | bytes 1572864 | tf_op jit(solution)/shard_map/reshape | solution.py:215
  118.4 1.6 %convolution_subtract_fusion.1 = f32[32,6144]{1,0:T(8,128)S(1)} fusion(f32[32,6144]{1,0:T(8,128)} %reshape.61, f32[32,32]{1,0:T(8,128)S(1)} %fusion.33, f32[32,6144]{1,0:T(8,128)S(1)} %reshape.56), kind=kOutput, calls=%fused_computation.5 | convolution fusion | flops 37945344 | bytes 2363392 | tf_op jit(solution)/shard_map/dot_general | solution.py:202
  120.0 1.4 %reshape.62 = f32[32,3,4,4,128]{4,3,2,1,0:T(4,128)} reshape(f32[32,6144]{1,0:T(8,128)S(1)} %convolution_subtract_fusion.1) | data formatting | bytes 1572864 | tf_op jit(solution)/shard_map/reshape | solution.py:215
  122.0 1.4 %reshape.60 = f32[32,3,4,4,128]{4,3,2,1,0:T(4,128)} reshape(f32[32,6144]{1,0:T(8,128)S(1)} %convolution_add_fusion.2) | data formatting | bytes 1572864 | tf_op jit(solution)/shard_map/reshape | solution.py:215
  (63 shorter events, 17.9 us)
Async XLA Ops:
  0.6 34.0 %copy-start = (f32[1,1,128,128]{3,2,1,0:T(8,128)S(1)}, f32[1,1,128,128]{3,2,1,0:T(8,128)}, u32[]{:S(2)}) copy-start(f32[1,1,128,128]{3,2,1,0:T(8,128)} %param.16) | copy-start | bytes 196612
  1.9 31.5 %copy-start.13 = (f32[4,4,128]{2,1,0:T(4,128)S(1)}, f32[4,4,128]{2,1,0:T(4,128)}, u32[]{:S(2)}) copy-start(f32[4,4,128]{2,1,0:T(4,128)} %param.14) | copy-start | bytes 24580
  1.9 31.5 %copy-start.2 = (f32[32,3,4,4,128]{4,3,2,1,0:T(4,128)S(1)}, f32[32,3,4,4,128]{4,3,2,1,0:T(4,128)}, u32[]{:S(2)}) copy-start(f32[32,3,4,4,128]{4,3,2,1,0:T(4,128)} %param.12) | copy-start | bytes 2359300
  2.0 14.1 %collective-permute-start = (f32[32,3,2,4,128]{4,0,3,2,1:T(8,128)S(1)}, f32[32,3,2,4,128]{4,0,3,2,1:T(8,128)S(1)}, u32[]{:S(2)}, u32[]{:S(2)}) collective-permute-start(f32[32,3,2,4,128]{4,0,3,2,1:T(8,128)S(1)} %copy.115), channel_id=1, source_target_pairs={{4,0},{8,4},{12,8},{16,12},{20,16},{24,20},{28,24},{5,1},{9,5},{13... | collective-permute-start | bytes 1179656 | tf_op jit(solution)/shard_map/ppermute | solution.py:128
  4.2 20.6 %collective-permute-start.1 = (f32[32,3,2,4,128]{4,0,3,2,1:T(8,128)}, f32[32,3,2,4,128]{4,0,3,2,1:T(8,128)}, u32[]{:S(2)}, u32[]{:S(2)}) collective-permute-start(f32[32,3,2,4,128]{4,0,3,2,1:T(8,128)} %copy.114), channel_id=1, source_target_pairs={{0,4},{4,8},{8,12},{12,16},{16,20},{20,24},{24,28},{1,5},{5,9},{9,... | collective-permute-start | bytes 1179656 | tf_op jit(solution)/shard_map/ppermute | solution.py:127
  14.2 23.9 %copy-start.3 = (f32[32,3,4,4,128]{4,3,2,1,0:T(4,128)S(1)}, f32[32,3,4,4,128]{4,3,2,1,0:T(4,128)}, u32[]{:S(2)}) copy-start(f32[32,3,4,4,128]{4,3,2,1,0:T(4,128)} %param.15) | copy-start | bytes 2359300
  16.4 9.7 %copy-start.6 = (f32[32,3,2,4,128]{4,2,3,1,0:T(2,128)}, f32[32,3,2,4,128]{4,2,3,1,0:T(2,128)S(1)}, u32[]{:S(2)}) copy-start(f32[32,3,2,4,128]{4,2,3,1,0:T(2,128)S(1)} %copy.71) | copy-start | bytes 1179652
  26.1 0.8 copy-start.8
  26.9 14.9 %copy-start.1 = (f32[32,3,4,4,128]{4,3,2,1,0:T(4,128)S(1)}, f32[32,3,4,4,128]{4,3,2,1,0:T(4,128)}, u32[]{:S(2)}) copy-start(f32[32,3,4,4,128]{4,3,2,1,0:T(4,128)} %param.13) | copy-start | bytes 2359300
  28.1 16.0 %collective-permute-start.2 = (f32[32,3,8,2,128]{4,2,3,1,0:T(8,128)}, f32[32,3,8,2,128]{4,2,3,1,0:T(8,128)}, u32[]{:S(2)}, u32[]{:S(2)}) collective-permute-start(f32[32,3,8,2,128]{4,2,3,1,0:T(8,128)} %get-tuple-element.10), channel_id=1, source_target_pairs={{1,0},{2,1},{3,2},{5,4},{6,5},{7,6},{9,8},{10,9},{11,10},{13,12},{... | collective-permute-start | bytes 2359304 | tf_op jit(solution)/shard_map/ppermute | solution.py:128
  29.4 14.7 %collective-permute-start.3 = (f32[32,3,8,2,128]{4,2,3,1,0:T(8,128)}, f32[32,3,8,2,128]{4,2,3,1,0:T(8,128)}, u32[]{:S(2)}, u32[]{:S(2)}) collective-permute-start(f32[32,3,8,2,128]{4,2,3,1,0:T(8,128)} %get-tuple-element.9), channel_id=1, source_target_pairs={{0,1},{1,2},{2,3},{4,5},{5,6},{6,7},{8,9},{9,10},{10,11},{12,13},{... | collective-permute-start | bytes 2359304 | tf_op jit(solution)/shard_map/ppermute | solution.py:127
  41.8 8.2 %copy-start.7 = (f32[32,3,2,4,128]{4,2,3,1,0:T(2,128)S(1)}, f32[32,3,2,4,128]{4,2,3,1,0:T(2,128)}, u32[]{:S(2)}) copy-start(f32[32,3,2,4,128]{4,2,3,1,0:T(2,128)} %copy-done.6) | copy-start | bytes 1179652
  41.8 8.2 %copy-start.9 = (f32[32,3,2,4,128]{4,2,3,1,0:T(2,128)S(1)}, f32[32,3,2,4,128]{4,2,3,1,0:T(2,128)}, u32[]{:S(2)}) copy-start(f32[32,3,2,4,128]{4,2,3,1,0:T(2,128)} %copy-done.8) | copy-start | bytes 1179652
  50.0 7.9 %copy-start.12 = (f32[32,1024]{1,0:T(8,128)S(1)}, f32[32,1024]{1,0:T(8,128)}, u32[]{:S(2)}) copy-start(f32[32,1024]{1,0:T(8,128)} %param.17) | copy-start | bytes 393220
  56.8 53.4 %copy-start.4 = (f32[32,6144]{1,0:T(8,128)S(1)}, f32[32,6144]{1,0:T(8,128)}, u32[]{:S(2)}) copy-start(f32[32,6144]{1,0:T(8,128)} %reshape.57) | copy-start | bytes 2359300
  63.7 52.8 %copy-start.5 = (f32[32,6144]{1,0:T(8,128)S(1)}, f32[32,6144]{1,0:T(8,128)}, u32[]{:S(2)}) copy-start(f32[32,6144]{1,0:T(8,128)} %reshape.59) | copy-start | bytes 2359300
  107.9 8.1 %copy-start.11 = (f32[32,6144]{1,0:T(8,128)S(1)}, f32[32,6144]{1,0:T(8,128)}, u32[]{:S(2)}) copy-start(f32[32,6144]{1,0:T(8,128)} %reshape.63) | copy-start | bytes 2359300
  112.5 9.0 %copy-start.10 = (f32[32,6144]{1,0:T(8,128)S(1)}, f32[32,6144]{1,0:T(8,128)}, u32[]{:S(2)}) copy-start(f32[32,6144]{1,0:T(8,128)} %reshape.55) | copy-start | bytes 2359300
where the time goes:
time: 124 us; the launch traced here: 123 us
  Pallas kernels  32.2 us (26%)
  local copies, waits for them, and re-layouts  24.1 us (19%)
  matrix products  22 us (18%)
  other arithmetic  20.9 us (17%)
  starting transfers between devices  12.9 us (10%)
  waiting for transfers between devices  10.3 us (8%)
    pallas_call x1, Pallas kernels, sum_everywhere(): pl.pallas_call(functools.partial(sum_kernel, tuple(stages)), out_shape=(j...  32.2 us
    ppermute x2, starting transfers between devices, with_halo(): before = lax.ppermute(last, axis, up)  10.2 us
    ppermute x2, waiting for transfers between devices, with_halo(): before = lax.ppermute(last, axis, up)  8.37 us
    dot_general x6, matrix products, product(): return jnp.dot(left, right.T, precision=exact_mode)  7.4 us
    concatenate x2, other arithmetic, with_halo(): array = jnp.concatenate([before, array, after], axis=dim)  6.37 us
    add x2, other arithmetic, operate(): return (mass + 7.5) * center - 4.0 / 3.0 * nearby + 1.0 / 12.0 * farther  5.33 us
    another operation x3, other arithmetic, on_device(): lower = jnp.linalg.cholesky(gram_pq)  3.6 us
    reshape x2, local copies, waits for them, and re-layouts, along_lines(): return jnp.dot(lines, inverse.T, precision=close_mode).reshape(flat.shape)  3.4 us
  transfers between devices with their start and end apart: 4, of which 2 were waited for; matrix products, arithmetic and copies ran while one was open for 13% of the time, Pallas kernels for 0%

commit v1 on v0

v1 whole, which is shorter than its diff:
```python
import functools

import jax
import jax.numpy as jnp
from jax import lax
from jax.experimental import pallas as pl
from jax.experimental.pallas import tpu as pltpu
from jax.sharding import PartitionSpec as P

MESH = pl.DeviceIdType.MESH
EXACT = lax.Precision.HIGHEST
CLOSE = lax.Precision.HIGH
F32 = jnp.float32
WIDTH = 2
TILE = 8


def dot(a, b, precision):
    return lax.dot_general(a, b, (((1,), (0,)), ((), ())), precision=precision, preferred_element_type=F32)


def dot_t(a, b, precision):
    return lax.dot_general(a, b, (((1,), (1,)), ((), ())), precision=precision, preferred_element_type=F32)


def inverse_cholesky(gram):
    size = gram.shape[0]
    rows = lax.broadcasted_iota(jnp.int32, (size, size), 0)
    columns = lax.broadcasted_iota(jnp.int32, (size, size), 1)
    work = jnp.concatenate([gram, (rows == columns).astype(F32)], axis=1)
    below = lax.broadcasted_iota(jnp.int32, work.shape, 0)
    for j in range(size):
        scale = lax.rsqrt(work[j : j + 1, j : j + 1])
        row = work[j : j + 1, :] * scale
        column = work[:, j : j + 1] * scale
        work = jnp.where(below > j, work - column * row, jnp.where(below == j, row, work))
    return work[:, size:]


def step_kernel(
    axes, sizes,
    p_hbm, r_hbm, s_hbm, b_hbm, mass_ref, line_ref, factor_ref,
    s_out, r_out, d_out,
    p_nat, r_nat, s_nat, b_nat, stack, image, resid, up, down, left, right,
    parts, landed, full, lined_flat,
    load_sem, send_sem, recv_sem, rs_send, rs_recv, ag_send, ag_recv,
):
    (sub_axis, inner_axis), (n_sub, n_inner) = axes, sizes
    n = n_sub * n_inner
    K, comps, nodes, cz = p_hbm.shape
    cy = TILE // WIDTH
    cx = nodes // cy
    M = comps * nodes
    span = M * cz
    chunk = nodes * cz
    NC = factor_ref.shape[1]
    S = parts.shape[1]
    sub, inner = lax.axis_index(sub_axis), lax.axis_index(inner_axis)
    me = sub * n_inner + inner
    LR, LQ, B, PP = (pl.ds(i * K, K) for i in range(4))

    def device(linear):
        return {sub_axis: linear // n_inner, inner_axis: linear % n_inner}

    loads = []
    for i, (src, dst) in enumerate(((p_hbm, p_nat), (r_hbm, r_nat), (b_hbm, b_nat), (s_hbm, s_nat))):
        loads.append(pltpu.make_async_copy(src, dst, load_sem.at[i]))
        loads[-1].start()

    barrier = pltpu.get_barrier_semaphore()
    for d in range(1, n):
        pl.semaphore_signal(barrier, inc=1, device_id=device((me + d) % n), device_id_type=MESH)
    pl.semaphore_wait(barrier, n - 1)

    def remote(src, dst, ssem, rsem, target):
        return pltpu.make_async_remote_copy(
            src_ref=src, dst_ref=dst, send_sem=ssem, recv_sem=rsem, device_id=target, device_id_type=MESH
        )

    edge = WIDTH * cy

    @pl.when(sub < n_sub - 1)
    def _():
        for c in range(comps):
            remote(p_hbm.at[:, c, pl.ds(nodes - edge, edge)], up.at[c], send_sem.at[0, c], recv_sem.at[0, c],
                   {sub_axis: sub + 1}).start()

    @pl.when(sub > 0)
    def _():
        for c in range(comps):
            remote(p_hbm.at[:, c, pl.ds(0, edge)], down.at[c], send_sem.at[1, c], recv_sem.at[1, c],
                   {sub_axis: sub - 1}).start()

    def tile_rows(nat, m):
        flat = nat.reshape(K * M, cz)
        return flat[pl.ds(m, K, stride=M), :]

    def lanes(m, count=1):
        return pl.ds(m * cz, count * cz)

    loads[0].wait()
    for m in range(M):
        stack[PP, lanes(m)] = tile_rows(p_nat, m)

    @pl.when(inner < n_inner - 1)
    def _():
        for c in range(comps):
            for x in range(cx):
                remote(stack.at[PP, lanes((c * cx + x) * cy + cy - WIDTH, WIDTH)],
                       left.at[:, lanes((c * cx + x) * WIDTH, WIDTH)],
                       send_sem.at[2, c], recv_sem.at[2, c], {inner_axis: inner + 1}).start()

    @pl.when(inner > 0)
    def _():
        for c in range(comps):
            for x in range(cx):
                remote(stack.at[PP, lanes((c * cx + x) * cy, WIDTH)],
                       right.at[:, lanes((c * cx + x) * WIDTH, WIDTH)],
                       send_sem.at[3, c], recv_sem.at[3, c], {inner_axis: inner - 1}).start()

    @pl.when(sub == 0)
    def _():
        up[...] = jnp.zeros_like(up)

    @pl.when(sub == n_sub - 1)
    def _():
        down[...] = jnp.zeros_like(down)

    @pl.when(inner == 0)
    def _():
        left[...] = jnp.zeros_like(left)

    @pl.when(inner == n_inner - 1)
    def _():
        right[...] = jnp.zeros_like(right)

    line = line_ref[...]
    loads[1].wait()
    loads[2].wait()
    lined_flat[...] = dot_t(r_nat[...].reshape(K * M, cz), line, CLOSE)
    for m in range(M):
        stack[B, lanes(m)] = tile_rows(b_nat, m)
        resid[:, lanes(m)] = tile_rows(r_nat, m)
        stack[LR, lanes(m)] = lined_flat[pl.ds(m, K, stride=M), :]
    with_r = dot_t(resid[...], stack[pl.ds(2 * K, 2 * K), :], EXACT)

    lane = lax.broadcasted_iota(jnp.int32, (K, cz), 1)
    near, far = -4.0 / 3.0, 1.0 / 12.0

    def own(c, x, y):
        return stack[PP, lanes((c * cx + x) * cy + y)]

    for c in range(comps):
        for x in range(cx):
            for y in range(cy):
                centre = own(c, x, y)
                close, wide = [], []
                for off, group in ((1, close), (2, wide)):
                    group.append(jnp.where(lane >= off, pltpu.roll(centre, off, 1), 0.0))
                    group.append(jnp.where(lane < cz - off, pltpu.roll(centre, cz - off, 1), 0.0))
                    for sign in (off, -off):
                        if 0 <= x + sign < cx:
                            group.append(own(c, x + sign, y))
                        if 0 <= y + sign < cy:
                            group.append(own(c, x, y + sign))
                weight = mass_ref[pl.ds(x * cy + y, 1), :] + 7.5
                image[:, lanes((c * cx + x) * cy + y)] = (
                    weight * centre + near * functools.reduce(jnp.add, close) + far * functools.reduce(jnp.add, wide)
                )

    def wait_for(ref, sem):
        pltpu.make_async_copy(ref, ref, sem).wait()

    side = cx * WIDTH
    total = jnp.zeros((K, 4 * K), F32)
    for c in range(comps):
        @pl.when(sub > 0)
        def _():
            wait_for(up.at[c], recv_sem.at[0, c])

        @pl.when(sub < n_sub - 1)
        def _():
            wait_for(down.at[c], recv_sem.at[1, c])

        @pl.when(inner > 0)
        def _():
            wait_for(left.at[:, lanes(c * side, side)], recv_sem.at[2, c])

        @pl.when(inner < n_inner - 1)
        def _():
            wait_for(right.at[:, lanes(c * side, side)], recv_sem.at[3, c])

        above = up.at[c].reshape(K * edge, cz)
        under = down.at[c].reshape(K * edge, cz)

        def halo_tile(x, y):
            if x < 0:
                return above[pl.ds((x + WIDTH) * cy + y, K, stride=edge), :]
            if x >= cx:
                return under[pl.ds((x - cx) * cy + y, K, stride=edge), :]
            if y < 0:
                return left[:, lanes((c * cx + x) * WIDTH + y + WIDTH)]
            if y >= cy:
                return right[:, lanes((c * cx + x) * WIDTH + y - cy)]
            return None

        for x in range(cx):
            for y in range(cy):
                where = lanes((c * cx + x) * cy + y)
                value = image[:, where]
                for off, weight in ((1, near), (2, far)):
                    for sign in (off, -off):
                        for tile in (halo_tile(x + sign, y), halo_tile(x, y + sign)):
                            if tile is not None:
                                value = value + weight * tile
                image[:, where] = value

        tiles = jnp.concatenate([image[:, lanes(c * nodes + i)] for i in range(nodes)], axis=0)
        lined = dot_t(tiles, line, CLOSE)
        for i in range(nodes):
            stack[LQ, lanes(c * nodes + i)] = lined[i * K : (i + 1) * K]
        total = total + dot_t(image[:, pl.ds(c * chunk, chunk)], stack[:, pl.ds(c * chunk, chunk)], EXACT)

    both = jnp.concatenate([total[:, 2 * K : 3 * K], with_r[:, :K]], axis=0)
    mids = dot(both, factor_ref[...], EXACT)
    small = jnp.concatenate([total[:, : 2 * K], total[:, 3 * K :], with_r[:, K:]], axis=1)
    per_row = NC // cz
    for t in range(n):
        a, b = t // per_row, t % per_row
        for half in range(2):
            parts[t, pl.ds(half * TILE, TILE), :] = mids[
                half * K + a * TILE : half * K + (a + 1) * TILE, b * cz : (b + 1) * cz
            ]
    parts.reshape(n * S, cz)[pl.ds(2 * TILE, K, stride=S), :] = small

    for d in range(1, n):
        peer = (me + d) % n
        remote(parts.at[peer], landed.at[d], rs_send, rs_recv, device(peer)).start()
    wait_for(landed.at[pl.ds(1, n - 1)], rs_recv)
    mine = parts[me]
    for d in range(1, n):
        mine = mine + landed[d]
    full[me] = mine
    for d in range(1, n):
        remote(full.at[me], full.at[me], ag_send, ag_recv, device((me + d) % n)).start()
    wait_for(full.at[pl.ds(0, n - 1)], ag_recv)

    sums = full.reshape(n * S, cz)[pl.ds(2 * TILE, K, stride=S), :]
    lined_r_sum, lined_q_sum = sums[:, :K], sums[:, K : 2 * K]
    gram, proj_t = sums[:, 2 * K : 3 * K], sums[:, 3 * K :]
    mid = [
        jnp.concatenate(
            [
                jnp.concatenate([full[a * per_row + b, half * TILE : (half + 1) * TILE] for b in range(per_row)], axis=1)
                for a in range(K // TILE)
            ],
            axis=0,
        )
        for half in range(2)
    ]
    mid_q, mid_r = mid
    inv = inverse_cholesky(gram)

    def solve_t(rhs_t):
        return dot(dot_t(rhs_t, inv, EXACT), inv, EXACT)

    alpha_t = solve_t(proj_t)
    mid_new = mid_r - dot(alpha_t, mid_q, EXACT)
    last = dot_t(mid_new, jnp.concatenate([mid_q, factor_ref[...]], axis=0), EXACT)
    cross_t = lined_r_sum.T - dot_t(alpha_t, lined_q_sum, EXACT) + last[:, :K]
    beta_t = -solve_t(cross_t)
    mix = jnp.concatenate([-alpha_t, last[:, K:], beta_t], axis=1)

    loads[3].wait()
    s_flat = s_nat.reshape(K * M, cz)
    outs = [ref.reshape(K * M, cz) for ref in (s_out, r_out, d_out)]
    for c in range(comps):
        part = pl.ds(c * chunk, chunk)
        moved = dot(alpha_t, stack[PP, part], CLOSE)
        lowered = resid[:, part] - dot(alpha_t, image[:, part], CLOSE)
        turned = stack[LR, part] + dot(mix, stack[pl.ds(K, 3 * K), part], CLOSE)
        for i in range(nodes):
            rows = pl.ds(c * nodes + i, K, stride=M)
            cut = slice(i * cz, (i + 1) * cz)
            outs[0][rows, :] = s_flat[rows, :] + moved[:, cut]
            outs[1][rows, :] = lowered[:, cut]
            outs[2][rows, :] = turned[:, cut]

    for which, there, buffer in (
        (0, sub < n_sub - 1, up), (1, sub > 0, down), (2, inner < n_inner - 1, left), (3, inner > 0, right),
    ):
        @pl.when(there)
        def _(which=which, buffer=buffer):
            for c in range(comps):
                piece = buffer.at[c] if which < 2 else buffer.at[:, lanes(c * side, side)]
                wait_for(piece, send_sem.at[which, c])
    wait_for(landed.at[pl.ds(1, n - 1)], rs_send)
    wait_for(full.at[pl.ds(0, n - 1)], ag_send)


def on_device(axes, sizes, solution, residual, direction, mass, coarse_basis, line_inverse, coarse_factor):
    K, comps, cx, cy, cz = direction.shape
    n = sizes[0] * sizes[1]
    NC = coarse_factor.shape[1]
    nodes, M = cx * cy, comps * cx * cy
    assert K * NC == n * TILE * cz and K <= n and 4 * K <= cz and WIDTH * cy == TILE
    flat = (K, comps, nodes, cz)
    S = 3 * TILE
    vmem = pl.BlockSpec(memory_space=pltpu.VMEM)
    hbm = pl.BlockSpec(memory_space=pl.ANY)
    dma = pltpu.SemaphoreType.DMA
    natural = pltpu.VMEM(flat, F32)
    wide = pltpu.VMEM((K, M * cz), F32)
    outs = pl.pallas_call(
        functools.partial(step_kernel, axes, sizes),
        out_shape=[jax.ShapeDtypeStruct(flat, F32)] * 3,
        in_specs=[hbm] * 4 + [vmem] * 3,
        out_specs=[vmem] * 3,
        scratch_shapes=[
            natural, natural, natural, natural,
            pltpu.VMEM((4 * K, M * cz), F32), wide, wide,
            pltpu.VMEM((comps, K, WIDTH * cy, cz), F32), pltpu.VMEM((comps, K, WIDTH * cy, cz), F32),
            pltpu.VMEM((K, comps * cx * WIDTH * cz), F32), pltpu.VMEM((K, comps * cx * WIDTH * cz), F32),
            pltpu.VMEM((n, S, cz), F32), pltpu.VMEM((n, S, cz), F32), pltpu.VMEM((n, S, cz), F32),
            pltpu.VMEM((K * M, cz), F32),
            dma((4,)), dma((4, comps)), dma((4, comps)), dma, dma, dma, dma,
        ],
        compiler_params=pltpu.CompilerParams(collective_id=0, has_side_effects=True, vmem_limit_bytes=48 << 20),
    )(
        direction.reshape(flat), residual.reshape(flat), solution.reshape(flat), coarse_basis.reshape(flat),
        mass.reshape(nodes, cz), line_inverse.reshape(cz, cz), coarse_factor,
    )
    return tuple(out.reshape(direction.shape) for out in outs)


def solution(mesh):
    axes = tuple(mesh.axis_names)
    sizes = tuple(mesh.shape[a] for a in axes)
    sub, inner = axes
    field = P(None, None, sub, inner, None)
    return jax.shard_map(
        functools.partial(on_device, axes, sizes),
        mesh=mesh,
        in_specs=(field, field, field, P(sub, inner, None), field, P(sub, inner, None, None), P((sub, inner), None)),
        out_specs=(field, field, field),
        check_vma=False,
    )
```

time: 124 us -> 64.4 us (0.52)
  the two profiles are of different devices: /device:TPU:0 before, /device:TPU:29 now
where the time goes in v1:
time: 64.4 us; the launch traced here: 64 us
  Pallas kernels  53.7 us (83%)
  local copies, waits for them, and re-layouts  9.6 us (15%)
  between operations  0.66 us (1%)
    pallas_call x1, Pallas kernels, on_device(): pl.pallas_call(functools.partial(step_kernel, axes, sizes), out_shape=[ja...  53.7 us
    unnamed x17, local copies, waits for them, and re-layouts  9.6 us

profile of v1, /device:TPU:29, one launch (start us, length us, event | category | flops | bytes accessed | tf_op | source)
XLA Modules:
  0.0 64.0 jit_solution(9378578080279621502)
XLA Ops:
  0.6 0.0 copy-start.6
  0.6 0.7 %copy-done.6 = f32[4,4,128]{2,1,0:T(4,128)S(1)} copy-done((f32[4,4,128]{2,1,0:T(4,128)S(1)}, f32[4,4,128]{2,1,0:T(4,128)}, u32[]{:S(2)}) %copy-start.6) | copy-done | bytes 8216
  1.3 0.0 copy-start
  1.3 1.1 %copy-done = f32[32,3,4,4,128]{4,3,2,1,0:T(4,128)S(1)} copy-done((f32[32,3,4,4,128]{4,3,2,1,0:T(4,128)S(1)}, f32[32,3,4,4,128]{4,3,2,1,0:T(4,128)}, u32[]{:S(2)}) %copy-start) | copy-done | bytes 786456
  2.5 0.0 copy-start.1
  2.5 1.1 %copy-done.1 = f32[32,3,4,4,128]{4,3,2,1,0:T(4,128)S(1)} copy-done((f32[32,3,4,4,128]{4,3,2,1,0:T(4,128)S(1)}, f32[32,3,4,4,128]{4,3,2,1,0:T(4,128)}, u32[]{:S(2)}) %copy-start.1) | copy-done | bytes 786456
  3.6 0.0 copy-start.2
  3.6 1.1 %copy-done.2 = f32[32,3,4,4,128]{4,3,2,1,0:T(4,128)S(1)} copy-done((f32[32,3,4,4,128]{4,3,2,1,0:T(4,128)S(1)}, f32[32,3,4,4,128]{4,3,2,1,0:T(4,128)}, u32[]{:S(2)}) %copy-start.2) | copy-done | bytes 786456
  4.7 0.0 copy-start.3
  4.7 1.1 %copy-done.3 = f32[32,3,4,4,128]{4,3,2,1,0:T(4,128)S(1)} copy-done((f32[32,3,4,4,128]{4,3,2,1,0:T(4,128)S(1)}, f32[32,3,4,4,128]{4,3,2,1,0:T(4,128)}, u32[]{:S(2)}) %copy-start.3) | copy-done | bytes 786456
  5.9 0.0 copy-start.4
  5.9 0.9 %copy-done.4 = f32[32,1024]{1,0:T(8,128)S(1)} copy-done((f32[32,1024]{1,0:T(8,128)S(1)}, f32[32,1024]{1,0:T(8,128)}, u32[]{:S(2)}) %copy-start.4) | copy-done | bytes 131096
  6.8 0.0 copy-start.5
  6.8 0.8 %copy-done.5 = f32[1,1,128,128]{3,2,1,0:T(8,128)S(1)} copy-done((f32[1,1,128,128]{3,2,1,0:T(8,128)S(1)}, f32[1,1,128,128]{3,2,1,0:T(8,128)}, u32[]{:S(2)}) %copy-start.5) | copy-done | bytes 65560
  7.6 53.7 %shard_map.94 = (f32[32,3,16,128]{3,2,1,0:T(8,128)S(1)}, f32[32,3,16,128]{3,2,1,0:T(8,128)S(1)}, f32[32,3,16,128]{3,2,1,0:T(8,128)S(1)}) custom-call(f32[32,3,16,128]{3,2,1,0:T(8,128)S(1)} %bitcast.12, f32[32,3,16,128]{3,2,1,0:T(8,128)S(1)} %bitcast.13, f32[32,3,16,128]{3,2,1,0:T(8,128)S(1)} %bitcast.14, f32[32,3,16,128]{3,2,1,0:T(8,128)S(1)} %bitcast.15, ...), custom_call_target="tpu_custom_call" | custom-call | tf_op jit(solution)/shard_map/pallas_call | solution.py:314
  61.4 0.9 %copy.13 = f32[32,3,4,4,128]{4,3,2,1,0:T(4,128)} copy(f32[32,3,4,4,128]{4,3,2,1,0:T(4,128)S(1)} %bitcast.11) | data formatting | bytes 1572864
  62.2 0.9 %copy.14 = f32[32,3,4,4,128]{4,3,2,1,0:T(4,128)} copy(f32[32,3,4,4,128]{4,3,2,1,0:T(4,128)S(1)} %bitcast.10) | data formatting | bytes 1572864
  63.1 0.9 %copy.15 = f32[32,3,4,4,128]{4,3,2,1,0:T(4,128)} copy(f32[32,3,4,4,128]{4,3,2,1,0:T(4,128)S(1)} %bitcast.9) | data formatting | bytes 1572864
Async XLA Ops:
  0.6 0.7 %copy-start.6 = (f32[4,4,128]{2,1,0:T(4,128)S(1)}, f32[4,4,128]{2,1,0:T(4,128)}, u32[]{:S(2)}) copy-start(f32[4,4,128]{2,1,0:T(4,128)} %param.10) | copy-start | bytes 24580
  1.3 1.1 %copy-start = (f32[32,3,4,4,128]{4,3,2,1,0:T(4,128)S(1)}, f32[32,3,4,4,128]{4,3,2,1,0:T(4,128)}, u32[]{:S(2)}) copy-start(f32[32,3,4,4,128]{4,3,2,1,0:T(4,128)} %param.9) | copy-start | bytes 2359300
  2.5 1.1 %copy-start.1 = (f32[32,3,4,4,128]{4,3,2,1,0:T(4,128)S(1)}, f32[32,3,4,4,128]{4,3,2,1,0:T(4,128)}, u32[]{:S(2)}) copy-start(f32[32,3,4,4,128]{4,3,2,1,0:T(4,128)} %param.8) | copy-start | bytes 2359300
  3.6 1.1 %copy-start.2 = (f32[32,3,4,4,128]{4,3,2,1,0:T(4,128)S(1)}, f32[32,3,4,4,128]{4,3,2,1,0:T(4,128)}, u32[]{:S(2)}) copy-start(f32[32,3,4,4,128]{4,3,2,1,0:T(4,128)} %param.7) | copy-start | bytes 2359300
  4.7 1.1 %copy-start.3 = (f32[32,3,4,4,128]{4,3,2,1,0:T(4,128)S(1)}, f32[32,3,4,4,128]{4,3,2,1,0:T(4,128)}, u32[]{:S(2)}) copy-start(f32[32,3,4,4,128]{4,3,2,1,0:T(4,128)} %param.11) | copy-start | bytes 2359300
  5.9 0.9 %copy-start.4 = (f32[32,1024]{1,0:T(8,128)S(1)}, f32[32,1024]{1,0:T(8,128)}, u32[]{:S(2)}) copy-start(f32[32,1024]{1,0:T(8,128)} %factor_ref.1) | copy-start | bytes 393220
  6.8 0.8 %copy-start.5 = (f32[1,1,128,128]{3,2,1,0:T(8,128)S(1)}, f32[1,1,128,128]{3,2,1,0:T(8,128)}, u32[]{:S(2)}) copy-start(f32[1,1,128,128]{3,2,1,0:T(8,128)} %param.12) | copy-start | bytes 196612

commit v2 on v1

v2 whole, which is shorter than its diff:
```python
import functools

import jax
import jax.numpy as jnp
from jax import lax
from jax.experimental import pallas as pl
from jax.experimental.pallas import tpu as pltpu
from jax.sharding import PartitionSpec as P

MESH = pl.DeviceIdType.MESH
EXACT = lax.Precision.HIGHEST
CLOSE = lax.Precision.HIGH
F32 = jnp.float32
BF16 = jnp.bfloat16
WIDTH = 2
TILE = 8
SLOT = 2 * TILE
USED = TILE + 1


def dot(a, b, precision=None):
    return lax.dot_general(a, b, (((1,), (0,)), ((), ())), precision=precision, preferred_element_type=F32)


def dot_t(a, b, precision=None):
    return lax.dot_general(a, b, (((1,), (1,)), ((), ())), precision=precision, preferred_element_type=F32)


def split(x):
    high = x.astype(BF16)
    return high, (x - high.astype(F32)).astype(BF16)


def fold(x, rows):
    return x[:rows] + x[rows:]


def four_lanes(x):
    high, low = split(x)
    return jnp.concatenate([high, low, high, low], axis=1)


def four_rows(x):
    high, low = split(x)
    return jnp.concatenate([high, high, low, low], axis=0)


def inverse_cholesky(gram):
    size = gram.shape[0]
    rows = lax.broadcasted_iota(jnp.int32, (size, size), 0)
    columns = lax.broadcasted_iota(jnp.int32, (size, size), 1)
    work = jnp.concatenate([gram, (rows == columns).astype(F32)], axis=1)
    below = lax.broadcasted_iota(jnp.int32, work.shape, 0)
    for j in range(size):
        scale = lax.rsqrt(work[j : j + 1, j : j + 1])
        row = work[j : j + 1, :] * scale
        column = work[:, j : j + 1] * scale
        work = jnp.where(below > j, work - column * row, jnp.where(below == j, row, work))
    return work[:, size:]


def step_kernel(
    axes, sizes,
    p_hbm, r_hbm, s_hbm, b_hbm, mass_hbm, line_hbm, factor_hbm,
    s_out, r_out, d_out,
    p_nat, r_nat, s_nat, b_nat, field, image, xb, qb, rb, fb, up, down, left, right,
    early_parts, early_landed, early_full, parts, landed, full, mass_ref, line_ref, factor_ref,
    load_sem, send_sem, recv_sem, sum_sem,
):
    (sub_axis, inner_axis), (n_sub, n_inner) = axes, sizes
    n = n_sub * n_inner
    K, comps, nodes, cz = p_hbm.shape
    cy = TILE // WIDTH
    cx = nodes // cy
    M = comps * nodes
    chunk = nodes * cz
    NC = factor_hbm.shape[1]
    per_row = NC // cz
    edge = WIDTH * cy
    side = cx * WIDTH
    sub, inner = lax.axis_index(sub_axis), lax.axis_index(inner_axis)
    me = sub * n_inner + inner
    LR, LQ, B, PP = 0, K, 4 * K, 5 * K
    LOW = 2 * K

    loads = []
    for i, (src, dst) in enumerate((
        (p_hbm, p_nat), (r_hbm, r_nat), (line_hbm, line_ref), (b_hbm, b_nat), (mass_hbm, mass_ref),
        (factor_hbm, factor_ref), (s_hbm, s_nat),
    )):
        loads.append(pltpu.make_async_copy(src, dst, load_sem.at[i]))
        loads[-1].start()

    subs, inners = [sub], [inner]
    for d in range(1, n_sub):
        subs.append(jnp.where(sub + d < n_sub, sub + d, sub + d - n_sub))
    for d in range(1, n_inner):
        inners.append(jnp.where(inner + d < n_inner, inner + d, inner + d - n_inner))
    peers = [
        (i * n_inner + j, a * n_inner + b, {sub_axis: a, inner_axis: b})
        for i, a in enumerate(subs) for j, b in enumerate(inners) if i or j
    ]

    barrier = pltpu.get_barrier_semaphore()
    for _, _, target in peers:
        pl.semaphore_signal(barrier, inc=1, device_id=target, device_id_type=MESH)
    pl.semaphore_wait(barrier, n - 1)

    def remote(src, dst, ssem, rsem, target):
        return pltpu.make_async_remote_copy(
            src_ref=src, dst_ref=dst, send_sem=ssem, recv_sem=rsem, device_id=target, device_id_type=MESH
        )

    def wait_for(ref, sem):
        pltpu.make_async_copy(ref, ref, sem).wait()

    def lanes(m, count=1):
        return pl.ds(m * cz, count * cz)

    def tile_rows(nat, m):
        return nat.reshape(K * M, cz)[pl.ds(m, K, stride=M), :]

    def put(ref, row, distance, where, value):
        high, low = split(value)
        ref[pl.ds(row, K), where] = high
        ref[pl.ds(row + distance, K), where] = low

    @pl.when(sub < n_sub - 1)
    def _():
        for c in range(comps):
            remote(p_hbm.at[:, c, pl.ds(nodes - edge, edge)], up.at[c], send_sem.at[0, c], recv_sem.at[0, c],
                   {sub_axis: sub + 1}).start()

    loads[0].wait()
    for m in range(M):
        field[:, lanes(m)] = tile_rows(p_nat, m)

    @pl.when(inner < n_inner - 1)
    def _():
        for c in range(comps):
            for x in range(cx):
                remote(field.at[:, lanes((c * cx + x) * cy + cy - WIDTH, WIDTH)],
                       left.at[:, lanes((c * cx + x) * WIDTH, WIDTH)],
                       send_sem.at[2, c], recv_sem.at[2, c], {inner_axis: inner + 1}).start()

    @pl.when(inner > 0)
    def _():
        for c in range(comps):
            for x in range(cx):
                remote(field.at[:, lanes((c * cx + x) * cy, WIDTH)],
                       right.at[:, lanes((c * cx + x) * WIDTH, WIDTH)],
                       send_sem.at[3, c], recv_sem.at[3, c], {inner_axis: inner - 1}).start()

    for buffer, alone in (
        (up, sub == 0), (down, sub == n_sub - 1), (left, inner == 0), (right, inner == n_inner - 1),
    ):
        @pl.when(alone)
        def _(buffer=buffer):
            buffer[...] = jnp.zeros_like(buffer)

    for load in loads[1:]:
        load.wait()
    for m in range(M):
        put(rb, 0, K, lanes(m), tile_rows(r_nat, m))
        put(xb, B, LOW, lanes(m), tile_rows(b_nat, m))
        put(xb, PP, LOW, lanes(m), field[:, lanes(m)])
    fh, fl = split(factor_ref[...])
    for i, half in enumerate((fh, fh, fl, fl)):
        fb[pl.ds(i * K, K), :] = half

    with_r = jnp.zeros((2 * K, 4 * K), F32)
    for c in range(comps):
        part = pl.ds(c * chunk, chunk)
        with_r = with_r + dot_t(rb[:, part], xb[pl.ds(B, 4 * K), part])
    with_r = fold(with_r, K)
    with_r = with_r[:, :LOW] + with_r[:, LOW:]

    def spread(mid, small, slots):
        for t in range(n):
            a, b = t // per_row, t % per_row
            slots[t, pl.ds(0, TILE), :] = mid[a * TILE : (a + 1) * TILE, b * cz : (b + 1) * cz]
        slots.reshape(n * SLOT, cz)[pl.ds(TILE, K, stride=SLOT), :] = small

    def scatter(slots, arriving, ssem, rsem):
        for d, peer, target in peers:
            remote(slots.at[peer, pl.ds(0, USED)], arriving.at[d, pl.ds(0, USED)], ssem, rsem, target).start()

    def gather(slots, arriving, whole, rsem, ssem, next_rsem):
        wait_for(arriving.at[pl.ds(1, n - 1), pl.ds(0, USED)], rsem)
        for rows in (pl.ds(0, TILE), pl.ds(TILE, 1)):
            mine = slots[me, rows]
            for d in range(1, n):
                mine = mine + arriving[d, rows]
            whole[me, rows] = mine
        for _, _, target in peers:
            remote(whole.at[me, pl.ds(0, USED)], whole.at[me, pl.ds(0, USED)], ssem, next_rsem, target).start()

    def collect(whole, rsem):
        wait_for(whole.at[pl.ds(0, n - 1), pl.ds(0, USED)], rsem)
        mid = jnp.concatenate(
            [
                jnp.concatenate([whole[a * per_row + b, pl.ds(0, TILE)] for b in range(per_row)], axis=1)
                for a in range(K // TILE)
            ],
            axis=0,
        )
        return mid, whole.reshape(n * SLOT, cz)[pl.ds(TILE, K, stride=SLOT), :]

    spread(
        dot(four_lanes(with_r[:, :K]), fb[...]),
        jnp.concatenate([with_r[:, K:], jnp.zeros((K, cz - K), F32)], axis=1),
        early_parts,
    )
    scatter(early_parts, early_landed, sum_sem.at[0], sum_sem.at[1])

    @pl.when(sub > 0)
    def _():
        for c in range(comps):
            remote(p_hbm.at[:, c, pl.ds(0, edge)], down.at[c], send_sem.at[1, c], recv_sem.at[1, c],
                   {sub_axis: sub - 1}).start()

    line_high, line_low = split(line_ref[...])
    line_both = jnp.concatenate([line_high, line_high], axis=1)

    def lined(source, c):
        high = jnp.concatenate([source[pl.ds(0, K), lanes(c * nodes + i)] for i in range(nodes)], axis=0)
        low = jnp.concatenate([source[pl.ds(K, K), lanes(c * nodes + i)] for i in range(nodes)], axis=0)
        return dot_t(jnp.concatenate([high, low], axis=1), line_both) + dot_t(high, line_low)

    lane = lax.broadcasted_iota(jnp.int32, (K, cz), 1)
    near, far = -4.0 / 3.0, 1.0 / 12.0

    def own(c, x, y):
        return field[:, lanes((c * cx + x) * cy + y)]

    for c in range(comps):
        turned = lined(rb, c)
        for i in range(nodes):
            put(xb, LR, LOW, lanes(c * nodes + i), turned[i * K : (i + 1) * K])
        for x in range(cx):
            for y in range(cy):
                centre = own(c, x, y)
                close, wide = [], []
                for off, group in ((1, close), (2, wide)):
                    group.append(jnp.where(lane >= off, pltpu.roll(centre, off, 1), 0.0))
                    group.append(jnp.where(lane < cz - off, pltpu.roll(centre, cz - off, 1), 0.0))
                    for sign in (off, -off):
                        if 0 <= x + sign < cx:
                            group.append(own(c, x + sign, y))
                        if 0 <= y + sign < cy:
                            group.append(own(c, x, y + sign))
                weight = mass_ref[pl.ds(x * cy + y, 1), :] + 7.5
                image[:, lanes((c * cx + x) * cy + y)] = (
                    weight * centre + near * functools.reduce(jnp.add, close) + far * functools.reduce(jnp.add, wide)
                )

    gather(early_parts, early_landed, early_full, sum_sem.at[1], sum_sem.at[2], sum_sem.at[3])

    total = jnp.zeros((2 * K, 8 * K), F32)
    for c in range(comps):
        for which, (there, piece) in enumerate((
            (sub > 0, up.at[c]), (sub < n_sub - 1, down.at[c]),
            (inner > 0, left.at[:, lanes(c * side, side)]), (inner < n_inner - 1, right.at[:, lanes(c * side, side)]),
        )):
            @pl.when(there)
            def _(which=which, piece=piece):
                wait_for(piece, recv_sem.at[which, c])

        above = up.at[c].reshape(K * edge, cz)
        under = down.at[c].reshape(K * edge, cz)

        def halo_tile(x, y):
            if x < 0:
                return above[pl.ds((x + WIDTH) * cy + y, K, stride=edge), :]
            if x >= cx:
                return under[pl.ds((x - cx) * cy + y, K, stride=edge), :]
            if y < 0:
                return left[:, lanes((c * cx + x) * WIDTH + y + WIDTH)]
            if y >= cy:
                return right[:, lanes((c * cx + x) * WIDTH + y - cy)]
            return None

        for x in range(cx):
            for y in range(cy):
                where = lanes((c * cx + x) * cy + y)
                value = image[:, where]
                for off, weight in ((1, near), (2, far)):
                    for sign in (off, -off):
                        for tile in (halo_tile(x + sign, y), halo_tile(x, y + sign)):
                            if tile is not None:
                                value = value + weight * tile
                put(qb, 0, K, where, value)

        turned = lined(qb, c)
        for i in range(nodes):
            put(xb, LQ, LOW, lanes(c * nodes + i), turned[i * K : (i + 1) * K])
        part = pl.ds(c * chunk, chunk)
        total = total + dot_t(qb[:, part], xb[:, part])

    total = fold(total, K)
    lines_q = total[:, :LOW] + total[:, LOW : 2 * LOW]
    rest_q = total[:, 2 * LOW : 3 * LOW] + total[:, 3 * LOW :]
    spread(
        dot(four_lanes(rest_q[:, :K]), fb[...]),
        jnp.concatenate([lines_q, rest_q[:, K:], jnp.zeros((K, cz - 3 * K), F32)], axis=1),
        parts,
    )
    scatter(parts, landed, sum_sem.at[4], sum_sem.at[5])
    gather(parts, landed, full, sum_sem.at[5], sum_sem.at[6], sum_sem.at[7])
    mid_r, sums_r = collect(early_full, sum_sem.at[3])
    mid_q, sums_q = collect(full, sum_sem.at[7])

    inv = inverse_cholesky(sums_q[:, 2 * K : 3 * K])

    def solve_t(rhs_t):
        return dot(dot_t(rhs_t, inv, EXACT), inv, EXACT)

    alpha_t = solve_t(sums_r[:, :K])
    mid_new = mid_r - dot(four_lanes(alpha_t), four_rows(mid_q))
    last = fold(dot_t(
        jnp.concatenate(split(mid_new), axis=0),
        jnp.concatenate([*split(mid_q), fb[pl.ds(0, K), :], fb[pl.ds(2 * K, K), :]], axis=0),
    ), K)
    crossed, coarse_t = last[:, :K] + last[:, K : 2 * K], last[:, 2 * K : 3 * K] + last[:, 3 * K :]
    cross_t = sums_q[:, :K].T - dot_t(alpha_t, sums_q[:, K : 2 * K], EXACT) + crossed
    beta_t = -solve_t(cross_t)

    (ah, al), (bh, bl), (ch, cl) = split(alpha_t), split(beta_t), split(coarse_t)
    none = jnp.zeros((K, K), BF16)
    unit = (lax.broadcasted_iota(jnp.int32, (K, K), 0) == lax.broadcasted_iota(jnp.int32, (K, K), 1)).astype(BF16)

    def table(rows):
        return jnp.concatenate([jnp.concatenate(row, axis=1) for row in rows], axis=0)

    on_fields = table([[ch, bh, ch, bh], [cl, bl, none, none], [none, ah, none, ah], [none, al, none, none]])
    on_lines = table([[unit, -ah, unit, -ah], [none, -al, none, none]])
    on_image = table([[ah, ah], [al, none]])

    s_flat, r_flat = (nat.reshape(K * M, cz) for nat in (s_nat, r_nat))
    outs = [ref.reshape(K * M, cz) for ref in (s_out, r_out, d_out)]
    for c in range(comps):
        part = pl.ds(c * chunk, chunk)
        mixed = dot(on_fields, xb[pl.ds(B, 4 * K), part])
        turned = fold(mixed[: 2 * K], K) + fold(dot(on_lines, xb[pl.ds(0, 4 * K), part]), K)
        moved = fold(mixed[2 * K :], K)
        drop = fold(dot(on_image, qb[:, part]), K)
        for i in range(nodes):
            rows = pl.ds(c * nodes + i, K, stride=M)
            cut = slice(i * cz, (i + 1) * cz)
            outs[0][rows, :] = s_flat[rows, :] + moved[:, cut]
            outs[1][rows, :] = r_flat[rows, :] - drop[:, cut]
            outs[2][rows, :] = turned[:, cut]

    for which, there, buffer in (
        (0, sub < n_sub - 1, up), (1, sub > 0, down), (2, inner < n_inner - 1, left), (3, inner > 0, right),
    ):
        @pl.when(there)
        def _(which=which, buffer=buffer):
            for c in range(comps):
                piece = buffer.at[c] if which < 2 else buffer.at[:, lanes(c * side, side)]
                wait_for(piece, send_sem.at[which, c])
    for i in (0, 2, 4, 6):
        wait_for(full.at[pl.ds(0, n - 1), pl.ds(0, USED)], sum_sem.at[i])


def write_kernel(*refs):
    count = len(refs) // 2
    sources, targets, sem = refs[:count], refs[count : 2 * count], refs[-1]
    copies = [pltpu.make_async_copy(a, b, sem.at[i]) for i, (a, b) in enumerate(zip(sources, targets))]
    for copy in copies:
        copy.start()
    for copy in copies:
        copy.wait()


def on_device(axes, sizes, solution, residual, direction, mass, coarse_basis, line_inverse, coarse_factor):
    K, comps, cx, cy, cz = direction.shape
    n = sizes[0] * sizes[1]
    NC = coarse_factor.shape[1]
    nodes, M = cx * cy, comps * cx * cy
    assert K * NC == n * TILE * cz and K <= n and 4 * K <= cz and WIDTH * cy == TILE
    flat = (K, comps, nodes, cz)
    vmem = pl.BlockSpec(memory_space=pltpu.VMEM)
    hbm = pl.BlockSpec(memory_space=pltpu.HBM)
    dma = pltpu.SemaphoreType.DMA
    natural = pltpu.VMEM(flat, F32)
    wide = pltpu.VMEM((K, M * cz), F32)
    across = pltpu.VMEM((comps, K, WIDTH * cy, cz), F32)
    beside = pltpu.VMEM((K, comps * cx * WIDTH * cz), F32)
    slots = pltpu.VMEM((n, SLOT, cz), F32)
    inputs = (
        direction.reshape(flat), residual.reshape(flat), solution.reshape(flat), coarse_basis.reshape(flat),
        mass.reshape(nodes, cz), line_inverse.reshape(cz, cz), coarse_factor,
    )
    outs = pl.pallas_call(
        functools.partial(step_kernel, axes, sizes),
        out_shape=[jax.ShapeDtypeStruct(flat, F32)] * 3,
        in_specs=[hbm] * 7,
        out_specs=[vmem] * 3,
        scratch_shapes=[
            natural, natural, natural, natural, wide, wide,
            pltpu.VMEM((8 * K, M * cz), BF16), pltpu.VMEM((2 * K, M * cz), BF16), pltpu.VMEM((2 * K, M * cz), BF16),
            pltpu.VMEM((4 * K, NC), BF16),
            across, across, beside, beside,
            slots, slots, slots, slots, slots, slots,
            pltpu.VMEM((nodes, cz), F32), pltpu.VMEM((cz, cz), F32), pltpu.VMEM(coarse_factor.shape, F32),
            dma((7,)), dma((4, comps)), dma((4, comps)), dma((8,)),
        ],
        compiler_params=pltpu.CompilerParams(collective_id=0, has_side_effects=True, vmem_limit_bytes=48 << 20),
    )(*[pltpu.with_memory_space_constraint(array, pltpu.HBM) for array in inputs])
    outs = pl.pallas_call(
        write_kernel,
        out_shape=[jax.ShapeDtypeStruct(flat, F32)] * 3,
        in_specs=[vmem] * 3,
        out_specs=[hbm] * 3,
        scratch_shapes=[dma((3,))],
        compiler_params=pltpu.CompilerParams(vmem_limit_bytes=1 << 20),
    )(*outs)
    return tuple(out.reshape(direction.shape) for out in outs)


def solution(mesh):
    axes = tuple(mesh.axis_names)
    sizes = tuple(mesh.shape[a] for a in axes)
    sub, inner = axes
    field = P(None, None, sub, inner, None)
    return jax.shard_map(
        functools.partial(on_device, axes, sizes),
        mesh=mesh,
        in_specs=(field, field, field, P(sub, inner, None), field, P(sub, inner, None, None), P((sub, inner), None)),
        out_specs=(field, field, field),
        check_vma=False,
    )
```

time: 64.4 us -> 51.4 us (0.80)
  the two profiles are of different devices: /device:TPU:29 before, /device:TPU:0 now
where the time goes in v2:
time: 51.4 us; the launch traced here: 51.2 us
  Pallas kernels  50.6 us (98%)
  between operations  0.64 us (1%)
    pallas_call x1, Pallas kernels, on_device(): pl.pallas_call(functools.partial(step_kernel, axes, sizes), out_shape=[ja...  49.2 us
    pallas_call x1, Pallas kernels, on_device(): pl.pallas_call(write_kernel, out_shape=[jax.ShapeDtypeStruct(flat, F32)]...  1.43 us

profile of v2, /device:TPU:0, one launch (start us, length us, event | category | flops | bytes accessed | tf_op | source)
XLA Modules:
  0.0 51.2 jit_solution(16095646112906608246)
XLA Ops:
  0.6 49.2 %shard_map.94 = (f32[32,3,16,128]{3,2,1,0:T(8,128)S(1)}, f32[32,3,16,128]{3,2,1,0:T(8,128)S(1)}, f32[32,3,16,128]{3,2,1,0:T(8,128)S(1)}) custom-call(f32[32,3,16,128]{3,2,1,0:T(8,128)} %bitcast.9, f32[32,3,16,128]{3,2,1,0:T(8,128)} %bitcast.10, f32[32,3,16,128]{3,2,1,0:T(8,128)} %bitcast.11, f32[32,3,16,128]{3,2,1,0:T(8,128)} %bitcast.12, ...), custom_call_target="tpu_custom_call" | custom-call | tf_op jit(solution)/shard_map/pallas_call | solution.py:395
  49.8 1.4 %shard_map.95 = (f32[32,3,16,128]{3,2,1,0:T(8,128)}, f32[32,3,16,128]{3,2,1,0:T(8,128)}, f32[32,3,16,128]{3,2,1,0:T(8,128)}) custom-call(f32[32,3,16,128]{3,2,1,0:T(8,128)S(1)} %get-tuple-element.9.refs_0_, f32[32,3,16,128]{3,2,1,0:T(8,128)S(1)} %get-tuple-element.10.refs_1_, f32[32,3,16,128]{3,2,1,0:T(8,128)S(1)} %get-tuple-element.11.refs_2_), custom_call_target="tpu_custom_call" | custom-call | tf_op jit(solution)/shard_map/pallas_call | solution.py:411

commit v3 on v2

v3 whole, which is shorter than its diff:
```python
import functools

import jax
import jax.numpy as jnp
from jax import lax
from jax.experimental import pallas as pl
from jax.experimental.pallas import tpu as pltpu
from jax.sharding import PartitionSpec as P

MESH = pl.DeviceIdType.MESH
EXACT = lax.Precision.HIGHEST
CLOSE = lax.Precision.HIGH
F32 = jnp.float32
BF16 = jnp.bfloat16
WIDTH = 2
TILE = 8
SLOT = 2 * TILE
USED = TILE + 1


def dot(a, b, precision=None):
    return lax.dot_general(a, b, (((1,), (0,)), ((), ())), precision=precision, preferred_element_type=F32)


def dot_t(a, b, precision=None):
    return lax.dot_general(a, b, (((1,), (1,)), ((), ())), precision=precision, preferred_element_type=F32)


def split(x):
    high = x.astype(BF16)
    return high, (x - high.astype(F32)).astype(BF16)


def fold(x, rows):
    return x[:rows] + x[rows:]


def four_lanes(x):
    high, low = split(x)
    return jnp.concatenate([high, low, high, low], axis=1)


def four_rows(x):
    high, low = split(x)
    return jnp.concatenate([high, high, low, low], axis=0)


def inverse_cholesky(gram):
    size = gram.shape[0]
    rows = lax.broadcasted_iota(jnp.int32, (size, size), 0)
    columns = lax.broadcasted_iota(jnp.int32, (size, size), 1)
    work = jnp.concatenate([gram, (rows == columns).astype(F32)], axis=1)
    below = lax.broadcasted_iota(jnp.int32, work.shape, 0)
    for j in range(size):
        scale = lax.rsqrt(work[j : j + 1, j : j + 1])
        row = work[j : j + 1, :] * scale
        column = work[:, j : j + 1] * scale
        work = jnp.where(below > j, work - column * row, jnp.where(below == j, row, work))
    return work[:, size:]


def step_kernel(
    axes, sizes,
    p_hbm, r_hbm, s_hbm, b_hbm, mass_hbm, line_hbm, factor_hbm,
    s_out, r_out, d_out,
    p_nat, r_nat, s_nat, b_nat, field, image, xb, qb, rb, fb, up, down, left, right,
    early, early_a, held, early_b, early_full, parts, landed, full, mass_ref, line_ref, factor_ref,
    load_sem, send_sem, recv_sem, sum_sem, ready_sem,
):
    (sub_axis, inner_axis), (n_sub, n_inner) = axes, sizes
    n = n_sub * n_inner
    K, comps, nodes, cz = p_hbm.shape
    cy = TILE // WIDTH
    cx = nodes // cy
    M = comps * nodes
    chunk = nodes * cz
    NC = factor_hbm.shape[1]
    per_row = NC // cz
    edge = WIDTH * cy
    side = cx * WIDTH
    sub, inner = lax.axis_index(sub_axis), lax.axis_index(inner_axis)
    me = inner * n_sub + sub
    LR, LQ, B, PP = 0, K, 4 * K, 6 * K
    travel = pl.ds(0, USED)

    loads = []
    for i, (src, dst) in enumerate((
        (p_hbm, p_nat), (r_hbm, r_nat), (line_hbm, line_ref), (b_hbm, b_nat), (mass_hbm, mass_ref),
        (factor_hbm, factor_ref), (s_hbm, s_nat),
    )):
        loads.append(pltpu.make_async_copy(src, dst, load_sem.at[i]))
        loads[-1].start()

    def around(index, count):
        return [index] + [jnp.where(index + d < count, index + d, index + d - count) for d in range(1, count)]

    subs, inners = around(sub, n_sub), around(inner, n_inner)
    lines = ((sub_axis, sub, n_sub), (inner_axis, inner, n_inner))

    def greet(sem_of, reach):
        for which, (axis, index, count) in enumerate(lines):
            if reach < count:
                @pl.when(index + reach < count)
                def _():
                    pl.semaphore_signal(sem_of(which), inc=1, device_id={axis: index + reach}, device_id_type=MESH)

                @pl.when(index >= reach)
                def _():
                    pl.semaphore_signal(sem_of(which), inc=1, device_id={axis: index - reach}, device_id_type=MESH)

    def heard(index, count, reach):
        return (index + reach < count).astype(jnp.int32) + (index >= reach).astype(jnp.int32)

    barrier = pltpu.get_barrier_semaphore()
    greet(lambda which: barrier, 1)
    pl.semaphore_wait(barrier, heard(sub, n_sub, 1) + heard(inner, n_inner, 1))

    rounds = []
    reach = 1
    while reach < max(n_sub, n_inner) - 1:
        rounds.append(reach)
        reach *= 2

    def listen(step):
        for which, (axis, index, count) in enumerate(lines):
            if rounds[step] < count - 1:
                pl.semaphore_wait(ready_sem.at[which, step], heard(index, count, rounds[step]))

    def say(step):
        for which, (axis, index, count) in enumerate(lines):
            if rounds[step] < count - 1:
                @pl.when(index + rounds[step] < count)
                def _():
                    pl.semaphore_signal(ready_sem.at[which, step], inc=1, device_id={axis: index + rounds[step]},
                                        device_id_type=MESH)

                @pl.when(index >= rounds[step])
                def _():
                    pl.semaphore_signal(ready_sem.at[which, step], inc=1, device_id={axis: index - rounds[step]},
                                        device_id_type=MESH)

    spoken = [0]

    def advance(last=False):
        while spoken[0] < len(rounds):
            listen(spoken[0])
            spoken[0] += 1
            if spoken[0] < len(rounds):
                say(spoken[0])
            if not last:
                break

    def remote(src, dst, ssem, rsem, target):
        return pltpu.make_async_remote_copy(
            src_ref=src, dst_ref=dst, send_sem=ssem, recv_sem=rsem, device_id=target, device_id_type=MESH
        )

    def wait_for(ref, sem):
        pltpu.make_async_copy(ref, ref, sem).wait()

    def lanes(m, count=1):
        return pl.ds(m * cz, count * cz)

    def tile_rows(nat, m):
        return nat.reshape(K * M, cz)[pl.ds(m, K, stride=M), :]

    def put(ref, row, distance, where, value):
        high, low = split(value)
        ref[pl.ds(row, K), where] = high
        ref[pl.ds(row + distance, K), where] = low

    @pl.when(sub < n_sub - 1)
    def _():
        for c in range(comps):
            remote(p_hbm.at[:, c, pl.ds(nodes - edge, edge)], up.at[c], send_sem.at[0, c], recv_sem.at[0, c],
                   {sub_axis: sub + 1}).start()

    def send_down(some):
        @pl.when(sub > 0)
        def _():
            for c in some:
                remote(p_hbm.at[:, c, pl.ds(0, edge)], down.at[c], send_sem.at[1, c], recv_sem.at[1, c],
                       {sub_axis: sub - 1}).start()

    if rounds:
        say(0)
    loads[0].wait()
    for m in range(M):
        value = tile_rows(p_nat, m)
        field[:, lanes(m)] = value
        put(xb, PP, K, lanes(m), value)

    @pl.when(inner < n_inner - 1)
    def _():
        for c in range(comps):
            for x in range(cx):
                remote(field.at[:, lanes((c * cx + x) * cy + cy - WIDTH, WIDTH)],
                       left.at[:, lanes((c * cx + x) * WIDTH, WIDTH)],
                       send_sem.at[2, c], recv_sem.at[2, c], {inner_axis: inner + 1}).start()

    @pl.when(inner > 0)
    def _():
        for c in range(comps):
            for x in range(cx):
                remote(field.at[:, lanes((c * cx + x) * cy, WIDTH)],
                       right.at[:, lanes((c * cx + x) * WIDTH, WIDTH)],
                       send_sem.at[3, c], recv_sem.at[3, c], {inner_axis: inner - 1}).start()

    for buffer, alone in (
        (up, sub == 0), (down, sub == n_sub - 1), (left, inner == 0), (right, inner == n_inner - 1),
    ):
        @pl.when(alone)
        def _(buffer=buffer):
            buffer[...] = jnp.zeros_like(buffer)

    for load in loads[1:]:
        load.wait()
    advance()
    for m in range(M):
        put(rb, 0, K, lanes(m), tile_rows(r_nat, m))
        put(xb, B, K, lanes(m), tile_rows(b_nat, m))
    fh, fl = split(factor_ref[...])
    for i, half in enumerate((fh, fh, fl, fl)):
        fb[pl.ds(i * K, K), :] = half
    advance()

    def pairs(x):
        x = x[:, :K] + x[:, K:]
        return [x[i : i + K] + x[i + K : i + 2 * K] for i in range(0, x.shape[0], 2 * K)]

    with_r = jnp.zeros((4 * K, 2 * K), F32)
    for c in range(comps):
        part = pl.ds(c * chunk, chunk)
        with_r = with_r + dot_t(xb[pl.ds(B, 4 * K), part], rb[:, part])
    rhs_r, proj = pairs(with_r)

    def spread(mid, small, slots):
        for t in range(n):
            a, b = t // per_row, t % per_row
            slots[t, pl.ds(0, TILE), :] = mid[a * TILE : (a + 1) * TILE, b * cz : (b + 1) * cz]
        slots.reshape(n * SLOT, cz)[pl.ds(TILE, K, stride=SLOT), :] = small

    def collect(whole):
        mid = jnp.concatenate(
            [
                jnp.concatenate([whole[a * per_row + b, pl.ds(0, TILE)] for b in range(per_row)], axis=1)
                for a in range(K // TILE)
            ],
            axis=0,
        )
        return mid, whole.reshape(n * SLOT, cz)[pl.ds(TILE, K, stride=SLOT), :]

    line_high, line_low = split(line_ref[...])
    line_both = jnp.concatenate([line_high, line_high], axis=1)

    def lined(source, c):
        high = jnp.concatenate([source[pl.ds(0, K), lanes(c * nodes + i)] for i in range(nodes)], axis=0)
        low = jnp.concatenate([source[pl.ds(K, K), lanes(c * nodes + i)] for i in range(nodes)], axis=0)
        return dot_t(jnp.concatenate([high, low], axis=1), line_both) + dot_t(high, line_low)

    lane = lax.broadcasted_iota(jnp.int32, (K, cz), 1)
    near, far = -4.0 / 3.0, 1.0 / 12.0

    def own(c, x, y):
        return field[:, lanes((c * cx + x) * cy + y)]

    def against_field(c):
        part = pl.ds(c * chunk, chunk)
        return dot_t(xb[pl.ds(PP, 2 * K), part], qb[:, part])

    inside = jnp.zeros((2 * K, 2 * K), F32)
    for c in range(comps):
        turned = lined(rb, c)
        for i in range(nodes):
            put(xb, LR, 2 * K, lanes(c * nodes + i), turned[i * K : (i + 1) * K])
        for x in range(cx):
            for y in range(cy):
                centre = own(c, x, y)
                close, wide = [], []
                for off, group in ((1, close), (2, wide)):
                    group.append(jnp.where(lane >= off, pltpu.roll(centre, off, 1), 0.0))
                    group.append(jnp.where(lane < cz - off, pltpu.roll(centre, cz - off, 1), 0.0))
                    for sign in (off, -off):
                        if 0 <= x + sign < cx:
                            group.append(own(c, x + sign, y))
                        if 0 <= y + sign < cy:
                            group.append(own(c, x, y + sign))
                weight = mass_ref[pl.ds(x * cy + y, 1), :] + 7.5
                value = (
                    weight * centre + near * functools.reduce(jnp.add, close) + far * functools.reduce(jnp.add, wide)
                )
                where = lanes((c * cx + x) * cy + y)
                image[:, where] = value
                put(qb, 0, K, where, value)
        inside = inside + against_field(c)
        advance()
    spread_mid_r = dot(four_lanes(rhs_r.T), fb[...])
    send_down(range(1))

    def arrived(c, which):
        there, piece = (
            (sub > 0, up.at[c]), (sub < n_sub - 1, down.at[c]),
            (inner > 0, left.at[:, lanes(c * side, side)]), (inner < n_inner - 1, right.at[:, lanes(c * side, side)]),
        )[which]

        @pl.when(there)
        def _():
            wait_for(piece, recv_sem.at[which, c])

    def outside(c, x, y, below):
        terms = []
        above, under = up.at[c].reshape(K * edge, cz), down.at[c].reshape(K * edge, cz)
        for off, weight in ((1, near), (2, far)):
            if below and x - off < 0:
                terms.append(weight * above[pl.ds((x - off + WIDTH) * cy + y, K, stride=edge), :])
            if below and y - off < 0:
                terms.append(weight * left[:, lanes((c * cx + x) * WIDTH + y - off + WIDTH)])
            if not below and x + off >= cx:
                terms.append(weight * under[pl.ds((x + off - cx) * cy + y, K, stride=edge), :])
            if not below and y + off >= cy:
                terms.append(weight * right[:, lanes((c * cx + x) * WIDTH + y + off - cy)])
        return functools.reduce(jnp.add, terms) if terms else None

    between = jnp.zeros((2 * K, 2 * K), F32)
    for c in range(comps):
        arrived(c, 2)
        arrived(c, 0)
        for x in range(cx):
            for y in range(cy):
                where = lanes((c * cx + x) * cy + y)
                value = outside(c, x, y, True)
                if value is None:
                    qb[:, where] = jnp.zeros((2 * K, cz), BF16)
                else:
                    image[:, where] = image[:, where] + value
                    put(qb, 0, K, where, value)
        between = between + against_field(c)
    (inside,), (between,) = pairs(inside), pairs(between)
    gram_part = inside + between + between.T
    spread(
        spread_mid_r, jnp.concatenate([gram_part, proj.T, jnp.zeros((K, cz - 2 * K), F32)], axis=1), early,
    )
    advance(last=True)
    for d, b in list(enumerate(inners))[1:]:
        remote(early.at[pl.ds(b * n_sub, n_sub), travel], early_a.at[d, :, travel], sum_sem.at[0], sum_sem.at[1],
               {inner_axis: b}).start()
    send_down(range(1, comps))

    def inner_sum():
        wait_for(early_a.at[pl.ds(1, n_inner - 1), :, travel], sum_sem.at[1])
        for s in range(n_sub):
            for rows in (pl.ds(0, TILE), pl.ds(TILE, 1)):
                value = early[inner * n_sub + s, rows]
                for d in range(1, n_inner):
                    value = value + early_a[d, s, rows]
                held[s, rows] = value
        for d, a in list(enumerate(subs))[1:]:
            remote(held.at[a, travel], early_b.at[d, travel], sum_sem.at[2], sum_sem.at[3], {sub_axis: a}).start()

    def sub_sum():
        wait_for(early_b.at[pl.ds(1, n_sub - 1), travel], sum_sem.at[3])
        for rows in (pl.ds(0, TILE), pl.ds(TILE, 1)):
            value = held[sub, rows]
            for d in range(1, n_sub):
                value = value + early_b[d, rows]
            early_full[me, rows] = value
        for a in subs[1:]:
            remote(early_full.at[me, travel], early_full.at[me, travel], sum_sem.at[4], sum_sem.at[5],
                   {sub_axis: a}).start()

    def spread_inner():
        wait_for(early_b.at[pl.ds(1, n_sub - 1), travel], sum_sem.at[5])
        block = pl.ds(inner * n_sub, n_sub)
        for b in inners[1:]:
            remote(early_full.at[block, travel], early_full.at[block, travel], sum_sem.at[6], sum_sem.at[7],
                   {inner_axis: b}).start()

    between_chunks = [inner_sum, sub_sum]
    total = jnp.zeros((6 * K, 2 * K), F32)
    for c in range(comps):
        arrived(c, 3)
        arrived(c, 1)
        for x in range(cx):
            for y in range(cy):
                where = lanes((c * cx + x) * cy + y)
                value = outside(c, x, y, False)
                kept = image[:, where]
                put(qb, 0, K, where, kept if value is None else kept + value)
        turned = lined(qb, c)
        for i in range(nodes):
            put(xb, LQ, 2 * K, lanes(c * nodes + i), turned[i * K : (i + 1) * K])
        part = pl.ds(c * chunk, chunk)
        total = total + dot_t(xb[pl.ds(0, 6 * K), part], qb[:, part])
        if c < comps - 1 and between_chunks:
            between_chunks.pop(0)()

    total = total[:, :K] + total[:, K:]
    lined_r_part, lined_q_part = (total[i : i + K] + total[i + 2 * K : i + 3 * K] for i in (0, K))
    rhs_q = total[4 * K : 5 * K] + total[5 * K :]
    spread(
        dot(four_lanes(rhs_q.T), fb[...]),
        jnp.concatenate([lined_r_part, lined_q_part, jnp.zeros((K, cz - 2 * K), F32)], axis=1),
        parts,
    )
    peers = [
        (j * n_sub + i, b * n_sub + a, {sub_axis: a, inner_axis: b})
        for i, a in enumerate(subs) for j, b in enumerate(inners) if i or j
    ]
    for d, peer, target in peers:
        remote(parts.at[peer, travel], landed.at[d, travel], sum_sem.at[8], sum_sem.at[9], target).start()
    for step in between_chunks:
        step()
    spread_inner()

    wait_for(landed.at[pl.ds(1, n - 1), travel], sum_sem.at[9])
    for rows in (pl.ds(0, TILE), pl.ds(TILE, 1)):
        mine = parts[me, rows]
        for d in range(1, n):
            mine = mine + landed[d, rows]
        full[me, rows] = mine
    for _, _, target in peers:
        remote(full.at[me, travel], full.at[me, travel], sum_sem.at[10], sum_sem.at[11], target).start()

    wait_for(early_full.at[pl.ds(0, n - n_sub), travel], sum_sem.at[7])
    mid_r, sums_r = collect(early_full)
    inv = inverse_cholesky(sums_r[:, :K])

    def solve_t(rhs_t):
        return dot(dot_t(rhs_t, inv, EXACT), inv, EXACT)

    alpha_t = solve_t(sums_r[:, K : 2 * K])
    ah, al = split(alpha_t)
    none = jnp.zeros((K, K), BF16)
    unit = (lax.broadcasted_iota(jnp.int32, (K, K), 0) == lax.broadcasted_iota(jnp.int32, (K, K), 1)).astype(BF16)

    def table(rows):
        return jnp.concatenate([jnp.concatenate(row, axis=1) for row in rows], axis=0)

    on_lines = table([[unit, -ah, unit, -ah], [none, -al, none, none]])
    on_pair = table([[ah, ah], [al, none]])
    s_flat, r_flat = (nat.reshape(K * M, cz) for nat in (s_nat, r_nat))
    outs = [ref.reshape(K * M, cz) for ref in (s_out, r_out, d_out)]
    for c in range(comps):
        part = pl.ds(c * chunk, chunk)
        image[:, part] = fold(dot(on_lines, xb[pl.ds(0, 4 * K), part]), K)
        moved = fold(dot(on_pair, xb[pl.ds(PP, 2 * K), part]), K)
        drop = fold(dot(on_pair, qb[:, part]), K)
        for i in range(nodes):
            rows = pl.ds(c * nodes + i, K, stride=M)
            cut = slice(i * cz, (i + 1) * cz)
            outs[0][rows, :] = s_flat[rows, :] + moved[:, cut]
            outs[1][rows, :] = r_flat[rows, :] - drop[:, cut]

    wait_for(landed.at[pl.ds(1, n - 1), travel], sum_sem.at[11])
    mid_q, sums_q = collect(full)
    mid_new = mid_r - dot(four_lanes(alpha_t), four_rows(mid_q))
    last = fold(dot_t(
        jnp.concatenate(split(mid_new), axis=0),
        jnp.concatenate([*split(mid_q), fb[pl.ds(0, K), :], fb[pl.ds(2 * K, K), :]], axis=0),
    ), K)
    crossed, coarse_t = last[:, :K] + last[:, K : 2 * K], last[:, 2 * K : 3 * K] + last[:, 3 * K :]
    cross_t = sums_q[:, :K] - dot(alpha_t, sums_q[:, K : 2 * K], EXACT) + crossed
    (bh, bl), (ch, cl) = split(-solve_t(cross_t)), split(coarse_t)
    on_fields = table([[ch, ch, bh, bh], [cl, none, bl, none]])
    for c in range(comps):
        part = pl.ds(c * chunk, chunk)
        turned = image[:, part] + fold(dot(on_fields, xb[pl.ds(B, 4 * K), part]), K)
        for i in range(nodes):
            outs[2][pl.ds(c * nodes + i, K, stride=M), :] = turned[:, i * cz : (i + 1) * cz]

    for which, there, buffer in (
        (0, sub < n_sub - 1, up), (1, sub > 0, down), (2, inner < n_inner - 1, left), (3, inner > 0, right),
    ):
        @pl.when(there)
        def _(which=which, buffer=buffer):
            for c in range(comps):
                piece = buffer.at[c] if which < 2 else buffer.at[:, lanes(c * side, side)]
                wait_for(piece, send_sem.at[which, c])
    for i, count in ((0, n - n_sub), (2, n_sub - 1), (4, n_sub - 1), (6, n - n_sub), (8, n - 1), (10, n - 1)):
        wait_for(full.at[pl.ds(0, count), travel], sum_sem.at[i])


def write_kernel(*refs):
    count = len(refs) // 2
    sources, targets, sem = refs[:count], refs[count : 2 * count], refs[-1]
    copies = [pltpu.make_async_copy(a, b, sem.at[i]) for i, (a, b) in enumerate(zip(sources, targets))]
    for copy in copies:
        copy.start()
    for copy in copies:
        copy.wait()


def on_device(axes, sizes, solution, residual, direction, mass, coarse_basis, line_inverse, coarse_factor):
    K, comps, cx, cy, cz = direction.shape
    n = sizes[0] * sizes[1]
    NC = coarse_factor.shape[1]
    nodes, M = cx * cy, comps * cx * cy
    assert K * NC == n * TILE * cz and K <= n and 4 * K <= cz and WIDTH * cy == TILE
    flat = (K, comps, nodes, cz)
    vmem = pl.BlockSpec(memory_space=pltpu.VMEM)
    hbm = pl.BlockSpec(memory_space=pltpu.HBM)
    dma = pltpu.SemaphoreType.DMA
    natural = pltpu.VMEM(flat, F32)
    wide = pltpu.VMEM((K, M * cz), F32)
    across = pltpu.VMEM((comps, K, WIDTH * cy, cz), F32)
    beside = pltpu.VMEM((K, comps * cx * WIDTH * cz), F32)
    slots, line = (pltpu.VMEM((count, SLOT, cz), F32) for count in (n, sizes[0]))
    inputs = (
        direction.reshape(flat), residual.reshape(flat), solution.reshape(flat), coarse_basis.reshape(flat),
        mass.reshape(nodes, cz), line_inverse.reshape(cz, cz), coarse_factor,
    )
    outs = pl.pallas_call(
        functools.partial(step_kernel, axes, sizes),
        out_shape=[jax.ShapeDtypeStruct(flat, F32)] * 3,
        in_specs=[hbm] * 7,
        out_specs=[vmem] * 3,
        scratch_shapes=[
            natural, natural, natural, natural, wide, wide,
            pltpu.VMEM((8 * K, M * cz), BF16), pltpu.VMEM((2 * K, M * cz), BF16), pltpu.VMEM((2 * K, M * cz), BF16),
            pltpu.VMEM((4 * K, NC), BF16),
            across, across, beside, beside,
            slots, pltpu.VMEM((sizes[1], sizes[0], SLOT, cz), F32), line, line, slots, slots, slots, slots,
            pltpu.VMEM((nodes, cz), F32), pltpu.VMEM((cz, cz), F32), pltpu.VMEM(coarse_factor.shape, F32),
            dma((7,)), dma((4, comps)), dma((4, comps)), dma((12,)),
            pltpu.SemaphoreType.REGULAR((2, 8)),
        ],
        compiler_params=pltpu.CompilerParams(collective_id=0, has_side_effects=True, vmem_limit_bytes=48 << 20),
    )(*[pltpu.with_memory_space_constraint(array, pltpu.HBM) for array in inputs])
    outs = pl.pallas_call(
        write_kernel,
        out_shape=[jax.ShapeDtypeStruct(flat, F32)] * 3,
        in_specs=[vmem] * 3,
        out_specs=[hbm] * 3,
        scratch_shapes=[dma((3,))],
        compiler_params=pltpu.CompilerParams(vmem_limit_bytes=1 << 20),
    )(*outs)
    return tuple(out.reshape(direction.shape) for out in outs)


def solution(mesh):
    axes = tuple(mesh.axis_names)
    sizes = tuple(mesh.shape[a] for a in axes)
    sub, inner = axes
    field = P(None, None, sub, inner, None)
    return jax.shard_map(
        functools.partial(on_device, axes, sizes),
        mesh=mesh,
        in_specs=(field, field, field, P(sub, inner, None), field, P(sub, inner, None, None), P((sub, inner), None)),
        out_specs=(field, field, field),
        check_vma=False,
    )
```

time: 51.4 us -> 40.9 us (0.80)
  Pallas kernels: 50.6 us -> 40.1 us
    pallas_call x1, Pallas kernels: 49.2 us -> 38.7 us  [on_device(): pl.pallas_call(functools.partial(step_kernel, axes, sizes), out_shape=[ja...]
where the time goes in v3:
time: 40.9 us; the launch traced here: 40.7 us
  Pallas kernels  40.1 us (98%)
  between operations  0.64 us (2%)
    pallas_call x1, Pallas kernels, on_device(): pl.pallas_call(functools.partial(step_kernel, axes, sizes), out_shape=[ja...  38.7 us
    pallas_call x1, Pallas kernels, on_device(): pl.pallas_call(write_kernel, out_shape=[jax.ShapeDtypeStruct(flat, F32)]...  1.43 us

profile of v3, /device:TPU:0, one launch (start us, length us, event | category | flops | bytes accessed | tf_op | source)
XLA Modules:
  0.0 40.7 jit_solution(2555650793360553243)
XLA Ops:
  0.6 38.7 %shard_map.94 = (f32[32,3,16,128]{3,2,1,0:T(8,128)S(1)}, f32[32,3,16,128]{3,2,1,0:T(8,128)S(1)}, f32[32,3,16,128]{3,2,1,0:T(8,128)S(1)}) custom-call(f32[32,3,16,128]{3,2,1,0:T(8,128)} %bitcast.9, f32[32,3,16,128]{3,2,1,0:T(8,128)} %bitcast.10, f32[32,3,16,128]{3,2,1,0:T(8,128)} %bitcast.11, f32[32,3,16,128]{3,2,1,0:T(8,128)} %bitcast.12, ...), custom_call_target="tpu_custom_call" | custom-call | tf_op jit(solution)/shard_map/pallas_call | solution.py:512
  39.3 1.4 %shard_map.95 = (f32[32,3,16,128]{3,2,1,0:T(8,128)}, f32[32,3,16,128]{3,2,1,0:T(8,128)}, f32[32,3,16,128]{3,2,1,0:T(8,128)}) custom-call(f32[32,3,16,128]{3,2,1,0:T(8,128)S(1)} %get-tuple-element.9.refs_0_, f32[32,3,16,128]{3,2,1,0:T(8,128)S(1)} %get-tuple-element.10.refs_1_, f32[32,3,16,128]{3,2,1,0:T(8,128)S(1)} %get-tuple-element.11.refs_2_), custom_call_target="tpu_custom_call" | custom-call | tf_op jit(solution)/shard_map/pallas_call | solution.py:529

commit v4 on v3

v4 whole, which is shorter than its diff:
```python
import functools

import jax
import jax.numpy as jnp
from jax import lax
from jax.experimental import pallas as pl
from jax.experimental.pallas import tpu as pltpu
from jax.sharding import PartitionSpec as P

MESH = pl.DeviceIdType.MESH
EXACT = lax.Precision.HIGHEST
F32 = jnp.float32
BF16 = jnp.bfloat16
WIDTH = 2
TILE = 8
SLOT = 2 * TILE
USED = TILE + 1


def dot(a, b, precision=None):
    return lax.dot_general(a, b, (((1,), (0,)), ((), ())), precision=precision, preferred_element_type=F32)


def dot_t(a, b, precision=None):
    return lax.dot_general(a, b, (((1,), (1,)), ((), ())), precision=precision, preferred_element_type=F32)


def split(x):
    high = x.astype(BF16)
    return high, (x - high.astype(F32)).astype(BF16)


def fold(x, rows):
    return x[:rows] + x[rows:]


def inverse_cholesky(gram):
    size = gram.shape[0]
    rows = lax.broadcasted_iota(jnp.int32, (size, size), 0)
    columns = lax.broadcasted_iota(jnp.int32, (size, size), 1)
    work = jnp.concatenate([gram, (rows == columns).astype(F32)], axis=1)
    below = lax.broadcasted_iota(jnp.int32, work.shape, 0)
    for j in range(size):
        scale = lax.rsqrt(work[j : j + 1, j : j + 1])
        row = work[j : j + 1, :] * scale
        column = work[:, j : j + 1] * scale
        work = jnp.where(below > j, work - column * row, jnp.where(below == j, row, work))
    return work[:, size:]


def reaches(sizes):
    found = [1]
    while found[-1] < max(sizes) - 1:
        found.append(2 * found[-1])
    return [reach for reach in found if reach < max(sizes) - 1]


def step_kernel(
    axes, sizes,
    p_hbm, r_hbm, s_hbm, b_hbm, mass_hbm, line_hbm, factor_hbm,
    s_out, r_out, local, xf, table_out,
    p_nat, r_nat, s_nat, b_nat, field, image, xl, qb, rb, fb, up, down, left, right,
    early, early_a, held, early_b, early_full, rows_out, rows_in, rows_all, parts, landed, full,
    mass_ref, line_ref, factor_ref,
    load_sem, send_sem, sub_sem, side_sem, sum_sem, ready_sem,
):
    (sub_axis, inner_axis), (n_sub, n_inner) = axes, sizes
    n = n_sub * n_inner
    K, comps, nodes, cz = p_hbm.shape
    cy = TILE // WIDTH
    cx = nodes // cy
    M = comps * nodes
    chunk = nodes * cz
    NC = factor_hbm.shape[1]
    per_row = NC // cz
    edge = WIDTH * cy
    side = cx * WIDTH
    sub, inner = lax.axis_index(sub_axis), lax.axis_index(inner_axis)
    me = inner * n_sub + sub
    LR, LQ, B, PP = 0, K, 0, 2 * K
    travel = pl.ds(0, USED)
    tile, one = pl.ds(0, TILE), pl.ds(0, 1)

    def around(index, count):
        return [index] + [jnp.where(index + d < count, index + d, index + d - count) for d in range(1, count)]

    subs, inners = around(sub, n_sub), around(inner, n_inner)
    lines = ((sub_axis, sub, n_sub), (inner_axis, inner, n_inner))

    def greet(sem_of, reach):
        for which, (axis, index, count) in enumerate(lines):
            if reach < count:
                @pl.when(index + reach < count)
                def _():
                    pl.semaphore_signal(sem_of(which), inc=1, device_id={axis: index + reach}, device_id_type=MESH)

                @pl.when(index >= reach)
                def _():
                    pl.semaphore_signal(sem_of(which), inc=1, device_id={axis: index - reach}, device_id_type=MESH)

    def heard(index, count, reach):
        return (index + reach < count).astype(jnp.int32) + (index >= reach).astype(jnp.int32)

    barrier = pltpu.get_barrier_semaphore()
    greet(lambda which: barrier, 1)
    loads = []
    for i, (src, dst) in enumerate((
        (p_hbm, p_nat), (r_hbm, r_nat), (line_hbm, line_ref), (b_hbm, b_nat), (mass_hbm, mass_ref),
        (factor_hbm, factor_ref), (s_hbm, s_nat),
    )):
        loads.append(pltpu.make_async_copy(src, dst, load_sem.at[i]))
        loads[-1].start()
    pl.semaphore_wait(barrier, heard(sub, n_sub, 1) + heard(inner, n_inner, 1))

    rounds = reaches(sizes)

    def listen(step):
        for which, (axis, index, count) in enumerate(lines):
            if rounds[step] < count - 1:
                pl.semaphore_wait(ready_sem.at[which, step], heard(index, count, rounds[step]))

    def say(step):
        for which, (axis, index, count) in enumerate(lines):
            if rounds[step] < count - 1:
                @pl.when(index + rounds[step] < count)
                def _():
                    pl.semaphore_signal(ready_sem.at[which, step], inc=1, device_id={axis: index + rounds[step]},
                                        device_id_type=MESH)

                @pl.when(index >= rounds[step])
                def _():
                    pl.semaphore_signal(ready_sem.at[which, step], inc=1, device_id={axis: index - rounds[step]},
                                        device_id_type=MESH)

    spoken = [0]

    def advance(last=False):
        while spoken[0] < len(rounds):
            listen(spoken[0])
            spoken[0] += 1
            if spoken[0] < len(rounds):
                say(spoken[0])
            if not last:
                break

    def remote(src, dst, ssem, rsem, target):
        return pltpu.make_async_remote_copy(
            src_ref=src, dst_ref=dst, send_sem=ssem, recv_sem=rsem, device_id=target, device_id_type=MESH
        )

    def wait_for(ref, sem):
        pltpu.make_async_copy(ref, ref, sem).wait()

    def lanes(m, count=1):
        return pl.ds(m * cz, count * cz)

    def tile_rows(nat, m):
        return nat.reshape(K * M, cz)[pl.ds(m, K, stride=M), :]

    def put(ref, row, distance, where, value):
        high, low = split(value)
        ref[pl.ds(row, K), where] = high
        ref[pl.ds(row + distance, K), where] = low

    @pl.when(sub < n_sub - 1)
    def _():
        for c in range(comps):
            remote(p_hbm.at[:, c, pl.ds(nodes - edge, edge)], up.at[c], send_sem.at[0], sub_sem.at[0, c],
                   {sub_axis: sub + 1}).start()

    def send_down(some):
        @pl.when(sub > 0)
        def _():
            for c in some:
                remote(p_hbm.at[:, c, pl.ds(0, edge)], down.at[c], send_sem.at[1], sub_sem.at[1, c],
                       {sub_axis: sub - 1}).start()

    if rounds:
        say(0)
    loads[0].wait()
    for m in range(M):
        value = tile_rows(p_nat, m)
        field[:, lanes(m)] = value
        put(xf, PP, K, lanes(m), value)

    @pl.when(inner < n_inner - 1)
    def _():
        for c in range(comps):
            for x in range(cx):
                remote(field.at[:, lanes((c * cx + x) * cy + cy - WIDTH, WIDTH)],
                       left.at[:, lanes((c * cx + x) * WIDTH, WIDTH)],
                       send_sem.at[2], side_sem.at[0], {inner_axis: inner + 1}).start()

    @pl.when(inner > 0)
    def _():
        for c in range(comps):
            for x in range(cx):
                remote(field.at[:, lanes((c * cx + x) * cy, WIDTH)],
                       right.at[:, lanes((c * cx + x) * WIDTH, WIDTH)],
                       send_sem.at[3], side_sem.at[1], {inner_axis: inner - 1}).start()

    for buffer, alone in (
        (up, sub == 0), (down, sub == n_sub - 1), (left, inner == 0), (right, inner == n_inner - 1),
    ):
        @pl.when(alone)
        def _(buffer=buffer):
            buffer[...] = jnp.zeros_like(buffer)

    for load in loads[1:]:
        load.wait()
    advance()
    for m in range(M):
        put(rb, 0, K, lanes(m), tile_rows(r_nat, m))
        put(xf, B, K, lanes(m), tile_rows(b_nat, m))
    for i, half in enumerate(split(factor_ref[...])):
        fb[pl.ds(i * K, K), :] = half

    def through_factor(rhs_t):
        both = jnp.concatenate(split(rhs_t), axis=0)
        return fold(dot(both, fb[pl.ds(0, K), :]) + dot(both, fb[pl.ds(K, K), :]), K)
    advance()

    def pairs(x):
        x = x[:, :K] + x[:, K:]
        return [x[i : i + K] + x[i + K : i + 2 * K] for i in range(0, x.shape[0], 2 * K)]

    with_r = jnp.zeros((4 * K, 2 * K), F32)
    for c in range(comps):
        part = pl.ds(c * chunk, chunk)
        with_r = with_r + dot_t(xf[:, part], rb[:, part])
    rhs_r, proj = pairs(with_r)

    def spread(mid, slots):
        for t in range(n):
            a, b = t // per_row, t % per_row
            slots[t, tile, :] = mid[a * TILE : (a + 1) * TILE, b * cz : (b + 1) * cz]

    def collect(whole):
        return jnp.concatenate(
            [
                jnp.concatenate([whole[a * per_row + b, tile] for b in range(per_row)], axis=1)
                for a in range(K // TILE)
            ],
            axis=0,
        )

    def row_view(slots, at):
        depth = slots.shape[1]
        return slots.reshape(n * depth, cz).at[pl.ds(at, K, stride=depth), :]

    def padded(*blocks):
        return jnp.concatenate([*blocks, jnp.zeros((K, cz - K * len(blocks)), F32)], axis=1)

    line_high, line_low = split(line_ref[...])
    line_both = jnp.concatenate([line_high, line_high], axis=1)

    def put_lined(row, source, start, count):
        high = jnp.concatenate([source[pl.ds(0, K), lanes(start + i)] for i in range(count)], axis=0)
        low = jnp.concatenate([source[pl.ds(K, K), lanes(start + i)] for i in range(count)], axis=0)
        turned = dot_t(jnp.concatenate([high, low], axis=1), line_both) + dot_t(high, line_low)
        for i in range(count):
            put(xl, row, 2 * K, lanes(start + i), turned[i * K : (i + 1) * K])

    lane = lax.broadcasted_iota(jnp.int32, (K, cz), 1)
    near, far = -4.0 / 3.0, 1.0 / 12.0

    def own(c, x, y):
        return field[:, lanes((c * cx + x) * cy + y)]

    def against_field(c):
        part = pl.ds(c * chunk, chunk)
        return dot_t(xf[pl.ds(PP, 2 * K), part], qb[:, part])

    inside = jnp.zeros((2 * K, 2 * K), F32)
    for c in range(comps):
        put_lined(LR, rb, c * nodes, nodes)
        for x in range(cx):
            for y in range(cy):
                centre = own(c, x, y)
                close, wide = [], []
                for off, group in ((1, close), (2, wide)):
                    group.append(jnp.where(lane >= off, pltpu.roll(centre, off, 1), 0.0))
                    group.append(jnp.where(lane < cz - off, pltpu.roll(centre, cz - off, 1), 0.0))
                    for sign in (off, -off):
                        if 0 <= x + sign < cx:
                            group.append(own(c, x + sign, y))
                        if 0 <= y + sign < cy:
                            group.append(own(c, x, y + sign))
                weight = mass_ref[pl.ds(x * cy + y, 1), :] + 7.5
                value = (
                    weight * centre + near * functools.reduce(jnp.add, close) + far * functools.reduce(jnp.add, wide)
                )
                where = lanes((c * cx + x) * cy + y)
                image[:, where] = value
                put(qb, 0, K, where, value)
        inside = inside + against_field(c)
        advance()
    advance(last=True)
    spread(through_factor(rhs_r.T), early)
    for d, b in list(enumerate(inners))[1:]:
        remote(early.at[pl.ds(b * n_sub, n_sub)], early_a.at[d], sum_sem.at[0], sum_sem.at[1], {inner_axis: b}).start()

    @pl.when(sub < n_sub - 1)
    def _():
        wait_for(up, send_sem.at[0])
    send_down(range(1))

    def arrived(there, buffer, sem):
        @pl.when(there)
        def _():
            wait_for(buffer, sem)

    def outside(c, x, y, below):
        terms = []
        above, under = up.at[c].reshape(K * edge, cz), down.at[c].reshape(K * edge, cz)
        for off, weight in ((1, near), (2, far)):
            if below and x - off < 0:
                terms.append(weight * above[pl.ds((x - off + WIDTH) * cy + y, K, stride=edge), :])
            if below and y - off < 0:
                terms.append(weight * left[:, lanes((c * cx + x) * WIDTH + y - off + WIDTH)])
            if not below and x + off >= cx:
                terms.append(weight * under[pl.ds((x + off - cx) * cy + y, K, stride=edge), :])
            if not below and y + off >= cy:
                terms.append(weight * right[:, lanes((c * cx + x) * WIDTH + y + off - cy)])
        return functools.reduce(jnp.add, terms) if terms else None

    def inner_sum():
        wait_for(early_a.at[pl.ds(1, n_inner - 1)], sum_sem.at[1])
        for s in range(n_sub):
            value = early[inner * n_sub + s]
            for d in range(1, n_inner):
                value = value + early_a[d, s]
            held[s] = value
        for d, a in list(enumerate(subs))[1:]:
            remote(held.at[a], early_b.at[d], sum_sem.at[2], sum_sem.at[3], {sub_axis: a}).start()

    def sub_sum():
        wait_for(early_b.at[pl.ds(1, n_sub - 1)], sum_sem.at[3])
        value = held[sub]
        for d in range(1, n_sub):
            value = value + early_b[d]
        early_full[me] = value
        for a in subs[1:]:
            remote(early_full.at[me], early_full.at[me], sum_sem.at[4], sum_sem.at[5], {sub_axis: a}).start()

    def spread_inner():
        wait_for(early_b.at[pl.ds(1, n_sub - 1)], sum_sem.at[5])
        block = pl.ds(inner * n_sub, n_sub)
        for b in inners[1:]:
            remote(early_full.at[block], early_full.at[block], sum_sem.at[6], sum_sem.at[7], {inner_axis: b}).start()

    between = jnp.zeros((2 * K, 2 * K), F32)
    arrived(inner > 0, left, side_sem.at[0])
    for c in range(comps):
        arrived(sub > 0, up.at[c], sub_sem.at[0, c])
        for x in range(cx):
            for y in range(cy):
                where = lanes((c * cx + x) * cy + y)
                value = outside(c, x, y, True)
                if value is None:
                    qb[:, where] = jnp.zeros((2 * K, cz), BF16)
                else:
                    image[:, where] = image[:, where] + value
                    put(qb, 0, K, where, value)
        between = between + against_field(c)
    (inside,), (between,) = pairs(inside), pairs(between)
    gram_part = inside + between + between.T
    row_view(rows_out, 0)[...] = padded(gram_part, proj.T)
    peers = [
        (j * n_sub + i, b * n_sub + a, {sub_axis: a, inner_axis: b})
        for i, a in enumerate(subs) for j, b in enumerate(inners) if i or j
    ]
    inner_sum()
    for d, peer, target in peers:
        remote(rows_out.at[peer, one], rows_in.at[d, one], sum_sem.at[12], sum_sem.at[13], target).start()
    send_down(range(1, comps))

    def row_sum():
        wait_for(rows_in.at[pl.ds(1, n - 1), one], sum_sem.at[13])
        value = rows_out[me, one]
        for d in range(1, n):
            value = value + rows_in[d, one]
        rows_all[me, one] = value
        for _, _, target in peers:
            remote(rows_all.at[me, one], rows_all.at[me, one], sum_sem.at[14], sum_sem.at[15], target).start()

    def image_terms(c, rows):
        for x in rows:
            for y in range(cy):
                where = lanes((c * cx + x) * cy + y)
                value = outside(c, x, y, False)
                kept = image[:, where]
                put(qb, 0, K, where, kept if value is None else kept + value)
        start, count = c * nodes + rows[0] * cy, len(rows) * cy
        put_lined(LQ, qb, start, count)
        part = lanes(start, count)
        return dot_t(xl[:, part], qb[:, part]), dot_t(qb[:, part], xf[pl.ds(B, 2 * K), part])

    total, rhs_q = jnp.zeros((4 * K, 2 * K), F32), jnp.zeros((2 * K, 2 * K), F32)
    arrived(inner < n_inner - 1, right, side_sem.at[1])
    for c in range(comps):
        more, more_rhs = image_terms(c, range(cx - WIDTH))
        total, rhs_q = total + more, rhs_q + more_rhs
    for c in range(comps):
        arrived(sub < n_sub - 1, down.at[c], sub_sem.at[1, c])
        more, more_rhs = image_terms(c, range(cx - WIDTH, cx))
        total, rhs_q = total + more, rhs_q + more_rhs
        if c == comps - 2:
            sub_sum()
            row_sum()

    total = total[:, :K] + total[:, K:]
    lined_r_part, lined_q_part = (total[i : i + K] + total[i + 2 * K : i + 3 * K] for i in (0, K))
    rhs_q = fold(rhs_q, K)
    spread(through_factor(rhs_q[:, :K] + rhs_q[:, K:]), parts)
    row_view(parts, TILE)[...] = padded(lined_r_part, lined_q_part)
    for d, peer, target in peers:
        remote(parts.at[peer, travel], landed.at[d, travel], sum_sem.at[8], sum_sem.at[9], target).start()

    wait_for(rows_all.at[pl.ds(0, n - 1), one], sum_sem.at[15])
    sums_r = row_view(rows_all, 0)[...]
    inv = inverse_cholesky(sums_r[:, :K])


    wait_for(landed.at[pl.ds(1, n - 1), travel], sum_sem.at[9])
    for rows in (tile, pl.ds(TILE, 1)):
        value = parts[me, rows]
        for d in range(1, n):
            value = value + landed[d, rows]
        full[me, rows] = value
    for _, _, target in peers:
        remote(full.at[me, travel], full.at[me, travel], sum_sem.at[10], sum_sem.at[11], target).start()
    spread_inner()

    alpha_t = dot(dot_t(sums_r[:, K : 2 * K], inv, EXACT), inv, EXACT)
    gram_inverse = dot(inv.T, inv, EXACT)
    ah, al = split(alpha_t)
    none = jnp.zeros((K, K), BF16)
    unit = (lax.broadcasted_iota(jnp.int32, (K, K), 0) == lax.broadcasted_iota(jnp.int32, (K, K), 1)).astype(BF16)

    def table(rows):
        return jnp.concatenate([jnp.concatenate(row, axis=1) for row in rows], axis=0)

    on_lines = table([[unit, -ah, unit, -ah], [none, -al, none, none]])
    on_pair = table([[ah, ah], [al, none]])
    s_flat, r_flat = (nat.reshape(K * M, cz) for nat in (s_nat, r_nat))
    outs = [ref.reshape(K * M, cz) for ref in (s_out, r_out)]
    for c in range(comps):
        part = pl.ds(c * chunk, chunk)
        local[:, part] = fold(dot(on_lines, xl[:, part]), K)
        moved = fold(dot(on_pair, xf[pl.ds(PP, 2 * K), part]), K)
        drop = fold(dot(on_pair, qb[:, part]), K)
        for i in range(nodes):
            rows = pl.ds(c * nodes + i, K, stride=M)
            cut = slice(i * cz, (i + 1) * cz)
            outs[0][rows, :] = s_flat[rows, :] + moved[:, cut]
            outs[1][rows, :] = r_flat[rows, :] - drop[:, cut]

    wait_for(early_full.at[pl.ds(0, n - n_sub)], sum_sem.at[7])
    mid_r = jnp.concatenate(split(collect(early_full)), axis=0)

    wait_for(full.at[pl.ds(0, n - 1), travel], sum_sem.at[11])
    mid_q, sums_q = jnp.concatenate(split(collect(full)), axis=0), row_view(full, TILE)[...]
    meet = dot_t(jnp.concatenate([mid_q, mid_r], axis=0), jnp.concatenate([mid_q, fb[...]], axis=0))
    from_q, from_r = fold(meet[: 2 * K], K), fold(meet[2 * K :], K)
    taken = dot(alpha_t, jnp.concatenate(
        [from_q[:, :K] + from_q[:, K : 2 * K] + sums_q[:, K : 2 * K], from_q[:, 2 * K : 3 * K] + from_q[:, 3 * K :]], axis=1,
    ), EXACT)
    cross_t = sums_q[:, :K] + from_r[:, :K] + from_r[:, K : 2 * K] - taken[:, :K]
    coarse_t = from_r[:, 2 * K : 3 * K] + from_r[:, 3 * K :] - taken[:, K:]
    (bh, bl), (ch, cl) = split(-dot(cross_t, gram_inverse, EXACT)), split(coarse_t)
    table_out[...] = table([[ch, ch, bh, bh], [cl, none, bl, none]])

    arrived(sub > 0, down, send_sem.at[1])
    arrived(inner < n_inner - 1, left, send_sem.at[2])
    arrived(inner > 0, right, send_sem.at[3])
    for i, count in ((0, n - n_sub), (2, n_sub - 1), (4, n_sub - 1), (6, n - n_sub)):
        wait_for(early_full.at[pl.ds(0, count)], sum_sem.at[i])
    for i in (12, 14):
        wait_for(rows_all.at[pl.ds(0, n - 1), one], sum_sem.at[i])
    for i in (8, 10):
        wait_for(full.at[pl.ds(0, n - 1), travel], sum_sem.at[i])


def write_kernel(s_in, r_in, local, xf, table, s_hbm, r_hbm, d_hbm, d_nat, sem):
    K, comps, nodes, cz = s_in.shape
    M = comps * nodes
    copies = [pltpu.make_async_copy(s_in, s_hbm, sem.at[0]), pltpu.make_async_copy(r_in, r_hbm, sem.at[1])]
    for copy in copies:
        copy.start()
    mix = table[...]
    flat = d_nat.reshape(K * M, cz)
    for c in range(comps):
        part = pl.ds(c * nodes * cz, nodes * cz)
        turned = local[:, part] + fold(dot(mix, xf[:, part]), K)
        for i in range(nodes):
            flat[pl.ds(c * nodes + i, K, stride=M), :] = turned[:, i * cz : (i + 1) * cz]
        copies.append(pltpu.make_async_copy(d_nat.at[:, c], d_hbm.at[:, c], sem.at[2 + c]))
        copies[-1].start()
    for copy in copies:
        copy.wait()


def on_device(axes, sizes, solution, residual, direction, mass, coarse_basis, line_inverse, coarse_factor):
    K, comps, cx, cy, cz = direction.shape
    n = sizes[0] * sizes[1]
    NC = coarse_factor.shape[1]
    nodes, M = cx * cy, comps * cx * cy
    assert K * NC == n * TILE * cz and K <= n and 4 * K <= cz and WIDTH * cy == TILE
    flat = (K, comps, nodes, cz)
    vmem = pl.BlockSpec(memory_space=pltpu.VMEM)
    hbm = pl.BlockSpec(memory_space=pltpu.HBM)
    dma = pltpu.SemaphoreType.DMA
    natural = pltpu.VMEM(flat, F32)
    wide = pltpu.VMEM((K, M * cz), F32)
    across = pltpu.VMEM((comps, K, WIDTH * cy, cz), F32)
    beside = pltpu.VMEM((K, comps * cx * WIDTH * cz), F32)
    slots = pltpu.VMEM((n, SLOT, cz), F32)
    tiles, line = (pltpu.VMEM((count, TILE, cz), F32) for count in (n, sizes[0]))
    inputs = (
        direction.reshape(flat), residual.reshape(flat), solution.reshape(flat), coarse_basis.reshape(flat),
        mass.reshape(nodes, cz), line_inverse.reshape(cz, cz), coarse_factor,
    )
    outs = pl.pallas_call(
        functools.partial(step_kernel, axes, sizes),
        out_shape=[
            jax.ShapeDtypeStruct(flat, F32), jax.ShapeDtypeStruct(flat, F32), jax.ShapeDtypeStruct((K, M * cz), F32),
            jax.ShapeDtypeStruct((4 * K, M * cz), BF16), jax.ShapeDtypeStruct((2 * K, 4 * K), BF16),
        ],
        in_specs=[hbm] * 7,
        out_specs=[vmem] * 5,
        scratch_shapes=[
            natural, natural, natural, natural, wide, wide,
            pltpu.VMEM((4 * K, M * cz), BF16), pltpu.VMEM((2 * K, M * cz), BF16), pltpu.VMEM((2 * K, M * cz), BF16),
            pltpu.VMEM((2 * K, NC), BF16),
            across, across, beside, beside,
            tiles, pltpu.VMEM((sizes[1], sizes[0], TILE, cz), F32), line, line, tiles, tiles, tiles, tiles,
            slots, slots, slots,
            pltpu.VMEM((nodes, cz), F32), pltpu.VMEM((cz, cz), F32), pltpu.VMEM(coarse_factor.shape, F32),
            dma((7,)), dma((4,)), dma((2, comps)), dma((2,)), dma((16,)),
            pltpu.SemaphoreType.REGULAR((2, max(len(reaches(sizes)), 1))),
        ],
        compiler_params=pltpu.CompilerParams(collective_id=0, has_side_effects=True, vmem_limit_bytes=40 << 20),
    )(*[pltpu.with_memory_space_constraint(array, pltpu.HBM) for array in inputs])
    outs = pl.pallas_call(
        write_kernel,
        out_shape=[jax.ShapeDtypeStruct(flat, F32)] * 3,
        in_specs=[vmem] * 5,
        out_specs=[hbm] * 3,
        scratch_shapes=[natural, dma((2 + comps,))],
        compiler_params=pltpu.CompilerParams(vmem_limit_bytes=8 << 20),
    )(*outs)
    return tuple(out.reshape(direction.shape) for out in outs)


def solution(mesh):
    axes = tuple(mesh.axis_names)
    sizes = tuple(mesh.shape[a] for a in axes)
    sub, inner = axes
    field = P(None, None, sub, inner, None)
    return jax.shard_map(
        functools.partial(on_device, axes, sizes),
        mesh=mesh,
        in_specs=(field, field, field, P(sub, inner, None), field, P(sub, inner, None, None), P((sub, inner), None)),
        out_specs=(field, field, field),
        check_vma=False,
    )
```

time: 40.9 us -> 39.8 us (0.973)
  Pallas kernels: 40.1 us -> 39 us
    pallas_call x1, Pallas kernels: 38.7 us -> 37.6 us  [on_device(): pl.pallas_call(functools.partial(step_kernel, axes, sizes), out_shape=[ja...]
where the time goes in v4:
time: 39.8 us; the launch traced here: 39.6 us
  Pallas kernels  39 us (98%)
  between operations  0.64 us (2%)
    pallas_call x1, Pallas kernels, on_device(): pl.pallas_call(functools.partial(step_kernel, axes, sizes), out_shape=[ja...  37.6 us
    pallas_call x1, Pallas kernels, on_device(): pl.pallas_call(write_kernel, out_shape=[jax.ShapeDtypeStruct(flat, F32)]...  1.44 us

profile of v4, /device:TPU:0, one launch (start us, length us, event | category | flops | bytes accessed | tf_op | source)
XLA Modules:
  0.0 39.6 jit_solution(15703903424702360553)
XLA Ops:
  0.6 37.6 %shard_map.94 = (f32[32,3,16,128]{3,2,1,0:T(8,128)S(1)}, f32[32,3,16,128]{3,2,1,0:T(8,128)S(1)}, f32[32,6144]{1,0:T(8,128)S(1)}, bf16[128,6144]{1,0:T(8,128)(2,1)S(1)}, bf16[64,128]{1,0:T(8,128)(2,1)S(1)}) custom-call(f32[32,3,16,128]{3,2,1,0:T(8,128)} %bitcast.9, f32[32,3,16,128]{3,2,1,0:T(8,128)} %bitcast.10, f32[32,3,16,128]{3,2,1,0:T(8,128)} %bitcast.11, ...), custom_call_target="tpu_custom_call" | custom-call | tf_op jit(solution)/shard_map/pallas_call | solution.py:524
  38.2 1.4 %shard_map.95 = (f32[32,3,16,128]{3,2,1,0:T(8,128)}, f32[32,3,16,128]{3,2,1,0:T(8,128)}, f32[32,3,16,128]{3,2,1,0:T(8,128)}) custom-call(f32[32,3,16,128]{3,2,1,0:T(8,128)S(1)} %get-tuple-element.11.s_in, f32[32,3,16,128]{3,2,1,0:T(8,128)S(1)} %get-tuple-element.12.r_in, f32[32,6144]{1,0:T(8,128)S(1)} %get-tuple-element.13.local, ...), custom_call_target="tpu_custom_call" | custom-call | tf_op jit(solution)/shard_map/pallas_call | solution.py:545

commit v5 on v4

--- a/solution.py
+++ b/solution.py
@@ -414,13 +414,8 @@
     rhs_q = fold(rhs_q, K)
     spread(through_factor(rhs_q[:, :K] + rhs_q[:, K:]), parts)
     row_view(parts, TILE)[...] = padded(lined_r_part, lined_q_part)
-    for d, peer, target in peers:
+    for d, peer, target in sorted(peers, key=lambda p: abs(p[0] % n_sub - n_sub // 2)):
         remote(parts.at[peer, travel], landed.at[d, travel], sum_sem.at[8], sum_sem.at[9], target).start()
-
-    wait_for(rows_all.at[pl.ds(0, n - 1), one], sum_sem.at[15])
-    sums_r = row_view(rows_all, 0)[...]
-    inv = inverse_cholesky(sums_r[:, :K])
-
 
     wait_for(landed.at[pl.ds(1, n - 1), travel], sum_sem.at[9])
     for rows in (tile, pl.ds(TILE, 1)):
@@ -432,6 +427,9 @@
         remote(full.at[me, travel], full.at[me, travel], sum_sem.at[10], sum_sem.at[11], target).start()
     spread_inner()
 
+    wait_for(rows_all.at[pl.ds(0, n - 1), one], sum_sem.at[15])
+    sums_r = row_view(rows_all, 0)[...]
+    inv = inverse_cholesky(sums_r[:, :K])
     alpha_t = dot(dot_t(sums_r[:, K : 2 * K], inv, EXACT), inv, EXACT)
     gram_inverse = dot(inv.T, inv, EXACT)
     ah, al = split(alpha_t)

time: 39.8 us -> 38.9 us (0.977)
  Pallas kernels: 39 us -> 38.2 us
    pallas_call x1, Pallas kernels: 37.6 us -> 36.7 us  [on_device(): pl.pallas_call(functools.partial(step_kernel, axes, sizes), out_shape=[ja...]
where the time goes in v5:
time: 38.9 us; the launch traced here: 38.8 us
  Pallas kernels  38.2 us (98%)
  between operations  0.64 us (2%)
    pallas_call x1, Pallas kernels, on_device(): pl.pallas_call(functools.partial(step_kernel, axes, sizes), out_shape=[ja...  36.7 us
    pallas_call x1, Pallas kernels, on_device(): pl.pallas_call(write_kernel, out_shape=[jax.ShapeDtypeStruct(flat, F32)]...  1.44 us

profile of v5, /device:TPU:0, one launch (start us, length us, event | category | flops | bytes accessed | tf_op | source)
XLA Modules:
  0.0 38.8 jit_solution(1335400861611153226)
XLA Ops:
  0.6 36.7 %shard_map.94 = (f32[32,3,16,128]{3,2,1,0:T(8,128)S(1)}, f32[32,3,16,128]{3,2,1,0:T(8,128)S(1)}, f32[32,6144]{1,0:T(8,128)S(1)}, bf16[128,6144]{1,0:T(8,128)(2,1)S(1)}, bf16[64,128]{1,0:T(8,128)(2,1)S(1)}) custom-call(f32[32,3,16,128]{3,2,1,0:T(8,128)} %bitcast.9, f32[32,3,16,128]{3,2,1,0:T(8,128)} %bitcast.10, f32[32,3,16,128]{3,2,1,0:T(8,128)} %bitcast.11, ...), custom_call_target="tpu_custom_call" | custom-call | tf_op jit(solution)/shard_map/pallas_call | solution.py:522
  37.4 1.4 %shard_map.95 = (f32[32,3,16,128]{3,2,1,0:T(8,128)}, f32[32,3,16,128]{3,2,1,0:T(8,128)}, f32[32,3,16,128]{3,2,1,0:T(8,128)}) custom-call(f32[32,3,16,128]{3,2,1,0:T(8,128)S(1)} %get-tuple-element.11.s_in, f32[32,3,16,128]{3,2,1,0:T(8,128)S(1)} %get-tuple-element.12.r_in, f32[32,6144]{1,0:T(8,128)S(1)} %get-tuple-element.13.local, ...), custom_call_target="tpu_custom_call" | custom-call | tf_op jit(solution)/shard_map/pallas_call | solution.py:543
